TPU v7x, 32 devices: a whole 2x2x4 slice. The times are simulated.
32 devices in a mesh: groups: 2 (over y), row: 4 (over z), col: 2 (over x), sub: 2 (over core).
Axes of the slice: x: 2, y: 2, z: 4, core: 2. Of those that a mesh axis runs over, the one named last changes fastest.
Arguments:
- matrix: float32 [16384, 8192], P(('groups', 'row'), ('col', 'sub')), parts along dimension 0, may hold values from -60 to 60
- basis_vectors: float32 [16384, 1024], P(('groups', 'row'), ('col', 'sub')), parts along dimension 0, may hold values from -0.0625 to 0.0625
- split_size: int32 [2], P('groups'), parts along dimension 0, may hold values from 256 to 767
Outputs:
- children: float32 [2, 2048, 1024], P('sub', ('groups', 'row'), 'col'), parts along dimension 1
There are 2 independent parts, one for each index of `groups`. A program takes and returns all parts, laid end to end along the dimension named above; each array names one. Nothing has to cross between parts.
Inputs may be any that keep to these rules, and one draw needn't show every extreme that they name: The second subspace has 1024 minus split_size vectors.
All inputs are finite; a program needn't handle non-finite values.
Results may differ from a plain program's by a relative error of at most 0.00011.
Values sent between devices are 32-bit elements; how exact they have to be, the bound alone decides.
A program may use at most 128 MiB of HBM per device.

v0:
```python
import functools

import jax
import jax.numpy as jnp
from jax import lax
from jax.experimental import pallas as pl
from jax.experimental.pallas import tpu as pltpu
from jax.sharding import PartitionSpec as P

MESH = pl.DeviceIdType.MESH
CHUNKS = 1


def gather_kernel(R, X, S, v, own, spread, lsem, xs, xr, zs, zr, ps, pr, fs, fr):
    r, x, s = lax.axis_index("row"), lax.axis_index("col"), lax.axis_index("sub")
    m, kd = v.shape
    piece = m // R

    def columns(cx, cs):
        return pl.ds(pl.multiple_of((cx * S + cs) * kd, kd), kd)

    peers = [{"col": lax.rem(x + d, X)} for d in range(1, X)]
    peers += [{"row": lax.rem(r + d, R)} for d in range(1, R)]
    peers += [{"sub": lax.rem(s + d, S)} for d in range(1, S)]
    barrier = pltpu.get_barrier_semaphore()
    for peer in peers:
        pl.semaphore_signal(barrier, inc=1, device_id=peer, device_id_type=MESH)
    pl.semaphore_wait(barrier, len(peers))

    mine = own.at[:, columns(x, s)]
    across, spreads, partner, forward = [], [], [], []
    for d in range(1, X):
        across.append(pltpu.make_async_remote_copy(
            v, mine, xs.at[d - 1], xr.at[d - 1],
            device_id={"col": lax.rem(x + d, X)}, device_id_type=MESH))
    for d in range(1, R):
        i = lax.rem(r + d, R)
        spreads.append(pltpu.make_async_remote_copy(
            v.at[pl.ds(pl.multiple_of(i * piece, piece), piece), :], spread.at[r],
            zs.at[d - 1], zr.at[d - 1],
            device_id={"row": i}, device_id_type=MESH))
    for d in range(1, S):
        partner.append(pltpu.make_async_remote_copy(
            v, mine, ps.at[d - 1], pr.at[d - 1],
            device_id={"sub": lax.rem(s + d, S)}, device_id_type=MESH))
    for copy in across + spreads + partner:
        copy.start()
    local = [
        pltpu.make_async_copy(v, mine, lsem.at[0]),
        pltpu.make_async_copy(
            v.at[pl.ds(pl.multiple_of(r * piece, piece), piece), :], spread.at[r], lsem.at[1]),
    ]
    for copy in local:
        copy.start()
    for d in range(1, X):
        across[d - 1].wait_recv()
        block = own.at[:, columns(lax.rem(x - d + X, X), s)]
        for e in range(1, S):
            copy = pltpu.make_async_remote_copy(
                block, block, fs.at[d - 1, e - 1], fr.at[d - 1, e - 1],
                device_id={"sub": lax.rem(s + e, S)}, device_id_type=MESH)
            copy.start()
            forward.append(copy)
    for copy in across:
        copy.wait_send()
    for copy in spreads + partner + forward:
        copy.wait()
    for copy in local:
        copy.wait()


def gather(v, R, X, S):
    m, kd = v.shape
    dma = pltpu.SemaphoreType.DMA
    return pl.pallas_call(
        functools.partial(gather_kernel, R, X, S),
        out_shape=(
            jax.ShapeDtypeStruct((m, kd * X * S), v.dtype),
            jax.ShapeDtypeStruct((R, m // R, kd), v.dtype),
        ),
        in_specs=[pl.BlockSpec(memory_space=pltpu.VMEM)],
        out_specs=(pl.BlockSpec(memory_space=pl.ANY), pl.BlockSpec(memory_space=pl.ANY)),
        scratch_shapes=[
            dma((2,)), dma((X - 1,)), dma((X - 1,)), dma((R - 1,)), dma((R - 1,)),
            dma((S - 1,)), dma((S - 1,)), dma((X - 1, S - 1)), dma((X - 1, S - 1)),
        ],
        compiler_params=pltpu.CompilerParams(collective_id=0, has_side_effects=True),
        cost_estimate=pl.CostEstimate(flops=0, bytes_accessed=100_000_000, transcendentals=0),
        name="gather",
    )(v)


def regroup_kernel(X, S, spread, mine, lsem, ss, rs):
    x, s = lax.axis_index("col"), lax.axis_index("sub")
    C = X * S
    k = x * S + s
    R, piece, kd = spread.shape
    per = R // C
    barrier = pltpu.get_barrier_semaphore()
    dests = [lax.rem(k + e, C) for e in range(C)]
    for j in dests[1:]:
        pl.semaphore_signal(
            barrier, inc=1, device_id={"col": j // S, "sub": lax.rem(j, S)}, device_id_type=MESH)
    pl.semaphore_wait(barrier, C - 1)
    target = mine.at[:, :, pl.ds(pl.multiple_of(k * kd, kd), kd)]
    copies = []
    for e in range(1, C):
        j = dests[e]
        copies.append(pltpu.make_async_remote_copy(
            spread.at[pl.ds(j * per, per)], target, ss.at[e - 1], rs.at[e - 1],
            device_id={"col": j // S, "sub": lax.rem(j, S)}, device_id_type=MESH))
    copies.append(pltpu.make_async_copy(spread.at[pl.ds(k * per, per)], target, lsem))
    for copy in copies:
        copy.start()
    for copy in copies:
        copy.wait()


def regroup(spread, X, S):
    R, piece, kd = spread.shape
    C = X * S
    dma = pltpu.SemaphoreType.DMA
    return pl.pallas_call(
        functools.partial(regroup_kernel, X, S),
        out_shape=jax.ShapeDtypeStruct((R // C, piece, kd * C), spread.dtype),
        in_specs=[pl.BlockSpec(memory_space=pltpu.VMEM)],
        out_specs=pl.BlockSpec(memory_space=pl.ANY),
        scratch_shapes=[dma, dma((C - 1,)), dma((C - 1,))],
        compiler_params=pltpu.CompilerParams(collective_id=1, has_side_effects=True),
        cost_estimate=pl.CostEstimate(flops=0, bytes_accessed=60_000_000, transcendentals=0),
        name="regroup",
    )(spread)


def project_kernel(R, X, S, p, out, acc, from_sub, from_col, from_row, res, from_pair,
                   a_s, a_r, b_s, b_r, c_s, c_r, d_s, d_r):
    r, x, s = lax.axis_index("row"), lax.axis_index("col"), lax.axis_index("sub")
    K = p.shape[0]
    rb, kd = K // R, K // (X * S)

    def rows(i):
        return pl.ds(pl.multiple_of(i * rb, rb), rb)

    def columns(cx, cs):
        return pl.ds(pl.multiple_of((cx * S + cs) * kd, kd), kd)

    def col(d):
        return lax.rem(x + d, X)

    peers = [{"col": col(d)} for d in range(1, X)]
    peers += [{"row": lax.rem(r + d, R)} for d in range(1, R)]
    peers += [{"sub": lax.rem(s + d, S)} for d in range(1, S)]
    barrier = pltpu.get_barrier_semaphore()
    for peer in peers:
        pl.semaphore_signal(barrier, inc=1, device_id=peer, device_id_type=MESH)
    pl.semaphore_wait(barrier, len(peers))

    order = list(range(1, X)) + [0]
    steps = list(range(1, R)) + [0]
    pair = {}
    for d in order:
        for e in range(1, S):
            other = lax.rem(s + e, S)
            pair[d, e] = pltpu.make_async_remote_copy(
                p.at[:, columns(col(d), other)], from_sub.at[e - 1, d],
                a_s.at[e - 1, d], a_r.at[e - 1, d],
                device_id={"sub": other}, device_id_type=MESH)
            pair[d, e].start()
    cross = {}
    for d in order:
        for e in range(1, S):
            pair[d, e].wait_recv()
        for q in steps:
            here = rows(lax.rem(r + q, R))
            total = p[here, columns(col(d), s)]
            for e in range(1, S):
                total = total + from_sub[e - 1, d, here, :]
            acc[d, here, :] = total
            if d > 0:
                cross[d, q] = pltpu.make_async_remote_copy(
                    acc.at[d, here], from_col.at[d - 1, here],
                    b_s.at[d - 1, q], b_r.at[d - 1, q],
                    device_id={"col": col(d)}, device_id_type=MESH)
                cross[d, q].start()
    along = []
    for q in steps:
        i = lax.rem(r + q, R)
        here = rows(i)
        total = acc[0, here, :]
        for d in range(1, X):
            cross[d, q].wait_recv()
            total = total + from_col[d - 1, here, :]
        if q > 0:
            acc[0, here, :] = total
            copy = pltpu.make_async_remote_copy(
                acc.at[0, here], from_row.at[q - 1], c_s.at[q - 1], c_r.at[q - 1],
                device_id={"row": i}, device_id_type=MESH)
            copy.start()
            along.append(copy)
    for q in range(1, R):
        along[q - 1].wait_recv()
        total = total + from_row[q - 1]
    res[...] = total
    last = []
    for e in range(1, S):
        copy = pltpu.make_async_remote_copy(
            res, from_pair.at[e - 1], d_s.at[e - 1], d_r.at[e - 1],
            device_id={"sub": lax.rem(s + e, S)}, device_id_type=MESH)
        copy.start()
        last.append(copy)
    out[:, pl.ds(pl.multiple_of(s * kd, kd), kd)] = total
    for e in range(1, S):
        last[e - 1].wait_recv()
        out[:, pl.ds(pl.multiple_of(lax.rem(s - e + S, S) * kd, kd), kd)] = from_pair[e - 1]
    for copy in list(pair.values()) + list(cross.values()) + along + last:
        copy.wait_send()


def project(partial, R, X, S):
    K = partial.shape[0]
    rb, kd = K // R, K // (X * S)
    dma = pltpu.SemaphoreType.DMA
    f32 = jnp.float32
    return pl.pallas_call(
        functools.partial(project_kernel, R, X, S),
        out_shape=jax.ShapeDtypeStruct((rb, S * kd), f32),
        in_specs=[pl.BlockSpec(memory_space=pltpu.VMEM)],
        out_specs=pl.BlockSpec(memory_space=pltpu.VMEM),
        scratch_shapes=[
            pltpu.VMEM((X, K, kd), f32),
            pltpu.VMEM((S - 1, X, K, kd), f32),
            pltpu.VMEM((X - 1, K, kd), f32),
            pltpu.VMEM((R - 1, rb, kd), f32),
            pltpu.VMEM((rb, kd), f32),
            pltpu.VMEM((S - 1, rb, kd), f32),
            dma((S - 1, X)), dma((S - 1, X)), dma((X - 1, R)), dma((X - 1, R)),
            dma((R - 1,)), dma((R - 1,)), dma((S - 1,)), dma((S - 1,)),
        ],
        compiler_params=pltpu.CompilerParams(collective_id=2, has_side_effects=True),
        cost_estimate=pl.CostEstimate(flops=0, bytes_accessed=60_000_000, transcendentals=0),
        name="project",
    )(partial)


def shards(matrix, basis_vectors, split_size):
    R = lax.axis_size("row")
    S = lax.axis_size("sub")
    C = lax.axis_size("col") * S
    m, kd = basis_vectors.shape
    K = kd * C
    n = matrix.shape[1]
    per = n // m
    piece = m // R
    own, spread = gather(basis_vectors, R, C // S, S)
    width = K // CHUNKS
    images = []
    for c in range(CHUNKS):
        part = lax.dot_general(
            matrix,
            own[:, c * width : (c + 1) * width],
            (((0,), (0,)), ((), ())),
            precision=lax.Precision.HIGH,
            preferred_element_type=jnp.float32,
        )
        if c == 0:
            part, spread = lax.optimization_barrier((part, spread))
        part = part.reshape(per, R, piece, width).transpose(1, 0, 2, 3).reshape(R * per * piece, width)
        images.append(lax.psum_scatter(part, "row", scatter_dimension=0, tiled=True))
    mine = regroup(spread, C // S, S).reshape(per * piece, K)
    partial_proj = jnp.concatenate(
        [
            lax.dot_general(
                mine,
                image,
                (((0,), (0,)), ((), ())),
                precision=lax.Precision.HIGH,
                preferred_element_type=jnp.float32,
            )
            for image in images
        ],
        axis=1,
    )
    child_block = project(partial_proj, R, C // S, S)
    row_ids = (
        jnp.arange(child_block.shape[0], dtype=jnp.int32)
        + lax.axis_index("row") * child_block.shape[0]
    )
    col_ids = (
        jnp.arange(child_block.shape[1], dtype=jnp.int32)
        + lax.axis_index("col") * child_block.shape[1]
    )
    leading = split_size[0]
    row_first = row_ids < leading
    col_first = col_ids < leading
    mask_one = row_first[:, None] & col_first[None, :]
    mask_two = jnp.logical_not(row_first)[:, None] & jnp.logical_not(col_first)[None, :]
    selected = jnp.where(lax.axis_index("sub") == 0, mask_one, mask_two)
    return jnp.where(selected, child_block, jnp.zeros((), jnp.float32))[None]


def solution(mesh):
    placed = (
        P(("groups", "row"), ("col", "sub")),
        P(("groups", "row"), ("col", "sub")),
        P("groups"),
    )
    return jax.shard_map(
        shards,
        mesh=mesh,
        in_specs=placed,
        out_specs=P("sub", ("groups", "row"), "col"),
        check_vma=False,
    )
```

profile of v0, /device:TPU:3, one launch (start us, length us, event | category | flops | bytes accessed | tf_op | source)
XLA Modules:
  0.0 297.2 jit_solution(3964352810595357344)
XLA Ops:
  6.5 0.0 reduce-scatter.2.cloned.1.call-start
  6.5 56.0 %gather.1 = (f32[2048,1024]{1,0:T(8,128)}, f32[4,512,256]{2,1,0:T(8,128)}) custom-call(f32[2048,256]{1,0:T(8,128)} %v.1), custom_call_target="tpu_custom_call" | custom-call | bytes 100000000 | tf_op jit(solution)/shard_map/gather/pallas_call | solution.py:75
  62.5 33.4 %fusion.4 = f32[2048,1024]{1,0:T(8,128)} fusion(f32[2048,2048]{1,0:T(8,128)} %param.3, f32[2048,1024]{1,0:T(8,128)} %get-tuple-element.9), kind=kOutput, calls=%fused_computation.7 | convolution fusion | flops 25769803776 | bytes 33554432 | tf_op jit(solution)/shard_map/dot_general | solution.py:258
  96.0 0.0 reduce-scatter.2.cloned.1.call-update
  96.0 27.0 %regroup.1 = f32[1,512,1024]{2,1,0:T(8,128)} custom-call(f32[4,512,256]{2,1,0:T(8,128)} %get-tuple-element.11.spread), custom_call_target="tpu_custom_call" | custom-call | bytes 60000000 | tf_op jit(solution)/shard_map/regroup/pallas_call | solution.py:123
  123.7 115.3 %reduce-scatter.2.cloned.1.call-done = f32[512,1024]{1,0:T(8,128)} async-done(((f32[2048,1024]{1,0:T(8,128)}), f32[512,1024]{1,0:T(8,128)}) %reduce-scatter.2.cloned.1.call-update) | async-done | bytes 2097168 | tf_op jit(solution)/shard_map/reduce_scatter | solution.py:268
  239.0 7.7 %fusion.p = f32[1024,1024]{1,0:T(8,128)} fusion(f32[512,1024]{1,0:T(8,128)} %reduce-scatter.2.cloned.1.call-done, f32[1,512,1024]{2,1,0:T(8,128)} %regroup.1), kind=kOutput, calls=%fused_computation | convolution fusion | flops 3221225472 | bytes 8388608 | tf_op jit(solution)/shard_map/dot_general | solution.py:272
  246.6 41.7 %project.1 = f32[256,512]{1,0:T(8,128)} custom-call(f32[1024,1024]{1,0:T(8,128)} %fusion.p), custom_call_target="tpu_custom_call" | custom-call | bytes 60000000 | tf_op jit(solution)/shard_map/project/pallas_call | solution.py:224
  288.4 2.0 select_bitcast_fusion
  (2 shorter events, 0.0 us)
Async XLA Ops:
  6.5 232.4 %reduce-scatter.2.cloned.1.call-start = ((), (), s32[]{:S(2)}) async-start(), calls=%async_computation.1 | async-start | bytes 10485760 | tf_op jit(solution)/shard_map/reduce_scatter | solution.py:268
Sparse Core Ops, SparseCore 0:
  96.1 142.8 reduce-scatter.1
where the time goes:
time: 299 us; the launch traced here: 297 us
  Pallas kernels  125 us (42%)
  waiting for transfers between devices  115 us (38%)
  matrix products  41.1 us (14%)
  between operations  14.1 us (5%)
    reduce_scatter x1, waiting for transfers between devices, shards(): lax.psum_scatter(part, 'row', scatter_dimension=0, tiled=True)  115 us
    pallas_call x1, Pallas kernels, gather(): pl.pallas_call(functools.partial(gather_kernel, R, X, S), out_shape=(jax....  56 us
    pallas_call x1, Pallas kernels, project(): pl.pallas_call(functools.partial(project_kernel, R, X, S), out_shape=jax....  41.7 us
    dot_general x1, matrix products, shards(): lax.dot_general(matrix, own[:, c * width:(c + 1) * width], (((0,), (0,)),...  33.4 us
    pallas_call x1, Pallas kernels, regroup(): pl.pallas_call(functools.partial(regroup_kernel, X, S), out_shape=jax.Sha...  27 us
    dot_general x1, matrix products, shards(): lax.dot_general(mine, image, (((0,), (0,)), ((), ())), precision=lax.Prec...  7.69 us
  transfers between devices with their start and end apart: 1, of which 1 were waited for; matrix products, arithmetic and copies ran while one was open for 0% of the time, Pallas kernels for 9%

commit v1 on v0

--- a/solution.py
+++ b/solution.py
@@ -132,7 +132,7 @@
     )(spread)
 
 
-def project_kernel(R, X, S, p, out, acc, from_sub, from_col, from_row, res, from_pair,
+def project_kernel(R, X, S, relative, p, out, acc, from_sub, from_col, from_row, res, from_pair,
                    a_s, a_r, b_s, b_r, c_s, c_r, d_s, d_r):
     r, x, s = lax.axis_index("row"), lax.axis_index("col"), lax.axis_index("sub")
     K = p.shape[0]
@@ -143,6 +143,14 @@
 
     def columns(cx, cs):
         return pl.ds(pl.multiple_of((cx * S + cs) * kd, kd), kd)
+
+    def held(i):
+        if not relative:
+            return rows(i)
+        return rows(lax.rem(i // S + X - x, X) * S + lax.rem(i, S))
+
+    def held_columns(d, cs):
+        return columns(d if relative else col(d), cs)
 
     def col(d):
         return lax.rem(x + d, X)
@@ -162,7 +170,7 @@
         for e in range(1, S):
             other = lax.rem(s + e, S)
             pair[d, e] = pltpu.make_async_remote_copy(
-                p.at[:, columns(col(d), other)], from_sub.at[e - 1, d],
+                p.at[:, held_columns(d, other)], from_sub.at[e - 1, d],
                 a_s.at[e - 1, d], a_r.at[e - 1, d],
                 device_id={"sub": other}, device_id_type=MESH)
             pair[d, e].start()
@@ -172,9 +180,10 @@
             pair[d, e].wait_recv()
         for q in steps:
             here = rows(lax.rem(r + q, R))
-            total = p[here, columns(col(d), s)]
+            there = held(lax.rem(r + q, R))
+            total = p[there, held_columns(d, s)]
             for e in range(1, S):
-                total = total + from_sub[e - 1, d, here, :]
+                total = total + from_sub[e - 1, d, there, :]
             acc[d, here, :] = total
             if d > 0:
                 cross[d, q] = pltpu.make_async_remote_copy(
@@ -216,13 +225,13 @@
         copy.wait_send()
 
 
-def project(partial, R, X, S):
+def project(partial, R, X, S, relative):
     K = partial.shape[0]
     rb, kd = K // R, K // (X * S)
     dma = pltpu.SemaphoreType.DMA
     f32 = jnp.float32
     return pl.pallas_call(
-        functools.partial(project_kernel, R, X, S),
+        functools.partial(project_kernel, R, X, S, relative),
         out_shape=jax.ShapeDtypeStruct((rb, S * kd), f32),
         in_specs=[pl.BlockSpec(memory_space=pltpu.VMEM)],
         out_specs=pl.BlockSpec(memory_space=pltpu.VMEM),
@@ -242,7 +251,272 @@
     )(partial)
 
 
-def shards(matrix, basis_vectors, split_size):
+def split(value):
+    high = value.astype(jnp.bfloat16)
+    return high, (value - high.astype(jnp.float32)).astype(jnp.bfloat16)
+
+
+def dot3(a_high, a_low, b_high, b_low, contract):
+    def one(a, b):
+        return lax.dot_general(a, b, ((contract, (0,)), ((), ())),
+                               preferred_element_type=jnp.float32)
+    return one(a_high, b_high) + (one(a_high, b_low) + one(a_low, b_high))
+
+
+def image_kernel(R, S, Q, v, a, vall, img, sbuf, ubuf, tbuf, abuf, ahi, alo, vhi, vlo, rhi, rlo,
+                 lsem, asem, os, orr, xs, xr, fs, fr, hs, hr, ts, tr):
+    z, x, s = lax.axis_index("row"), lax.axis_index("col"), lax.axis_index("sub")
+    c = x * S + s
+    m, kd = v.shape
+    half = S * kd
+    steps = m // abuf.shape[2]
+    w = m // steps
+    pw = w // Q
+    first = jnp.where(x == 0, c, 0)
+    last = jnp.where(x == 0, R - 1, c)
+    chained = (z >= first) & (z <= last)
+    diag = z == c
+    pair = (z == x * S + 1) & (s == 0)
+    relay = (z == x * S) & (s == 1 - x)
+    adds = (x == 1) & chained
+    weight = jnp.where(diag, 0.5, 1.0).astype(jnp.float32)
+    other = 1 - s
+
+    def rows(i, n):
+        return pl.ds(pl.multiple_of(i * n, n), n)
+
+    def block(hh, ss):
+        return pl.ds(pl.multiple_of((hh * S + ss) * kd, kd), kd)
+
+    barrier = pltpu.get_barrier_semaphore()
+    pl.semaphore_signal(barrier, inc=1, device_id={"sub": other}, device_id_type=MESH)
+    pl.semaphore_signal(barrier, inc=1, device_id={"col": 1 - x}, device_id_type=MESH)
+
+    @pl.when(z > 0)
+    def _():
+        for t in range(S):
+            pl.semaphore_signal(barrier, inc=1, device_id={"row": z - 1, "sub": t}, device_id_type=MESH)
+
+    @pl.when(z < R - 1)
+    def _():
+        for t in range(S):
+            pl.semaphore_signal(barrier, inc=1, device_id={"row": z + 1, "sub": t}, device_id_type=MESH)
+
+    def load(i):
+        return pltpu.make_async_copy(a.at[:, rows(i, w)], abuf.at[lax.rem(i, 2)], asem.at[lax.rem(i, 2)])
+
+    def mate():
+        return pltpu.make_async_remote_copy(
+            v, vall.at[:, block(0, s)], os, orr, device_id={"sub": other}, device_id_type=MESH)
+
+    def across(i):
+        return pltpu.make_async_remote_copy(
+            v.at[rows(i, w), :], vall.at[rows(i, w), block(1, s)], xs.at[i], xr.at[i],
+            device_id={"col": 1 - x}, device_id_type=MESH)
+
+    def share(i):
+        here = vall.at[rows(i, w), block(1, s)]
+        return pltpu.make_async_remote_copy(
+            here, here, fs.at[i], fr.at[i], device_id={"sub": other}, device_id_type=MESH)
+
+    def hand(i):
+        return pltpu.make_async_remote_copy(
+            vall.at[rows(i, w), pl.ds(half, half)], ubuf.at[rows(i, w), :], hs.at[i], hr.at[i],
+            device_id={"row": z + 1, "sub": 0}, device_id_type=MESH)
+
+    def origin(k):
+        return pltpu.make_async_remote_copy(
+            vall.at[rows(k, pw), pl.ds(0, half)], sbuf.at[rows(k, pw), :], ts.at[k], tr.at[k],
+            device_id={"row": z + 1}, device_id_type=MESH)
+
+    def onward(k):
+        return pltpu.make_async_remote_copy(
+            sbuf.at[rows(k, pw), :], sbuf.at[rows(k, pw), :], ts.at[k], tr.at[k],
+            device_id={"row": z + 1}, device_id_type=MESH)
+
+    own = pltpu.make_async_copy(v, vall.at[:, block(0, s)], lsem)
+    own.start()
+    load(0).start()
+    img[...] = jnp.zeros_like(img)
+    pl.semaphore_wait(barrier, 2 + S * ((z > 0).astype(jnp.int32) + (z < R - 1).astype(jnp.int32)))
+    mate().start()
+
+    def begin(i, carry):
+        across(i).start()
+        return carry
+
+    lax.fori_loop(0, steps, begin, 0)
+    own.wait()
+    mate().wait_recv()
+    source = (x == 0) & diag
+
+    @pl.when(source)
+    def _():
+        def send(k, carry):
+            origin(k).start()
+            return carry
+        lax.fori_loop(0, steps * Q, send, 0)
+
+    @pl.when(adds)
+    def _():
+        def prepare(i, carry):
+            high, low = split(vall[rows(i, w), pl.ds(0, half)])
+            vhi[rows(i, w), :] = high
+            vlo[rows(i, w), :] = low
+            return carry
+        lax.fori_loop(0, steps, prepare, 0)
+
+    def multiply(columns):
+        def tile(t, carry):
+            here = rows(t, w)
+            img[here, columns] += dot3(ahi[here, :], alo[here, :], rhi[...], rlo[...], (1,))
+            return carry
+        lax.fori_loop(0, steps, tile, 0)
+
+    def step(i, carry):
+        load(i).wait()
+
+        @pl.when(i < steps - 1)
+        def _():
+            load(i + 1).start()
+
+        def cut(t, carry):
+            high, low = split(abuf[lax.rem(i, 2), rows(t, w), :])
+            ahi[rows(t, w), :] = high
+            alo[rows(t, w), :] = low
+            return carry
+        lax.fori_loop(0, steps, cut, 0)
+
+        @pl.when(adds)
+        def _():
+            tbuf[...] = weight * dot3(ahi[...], alo[...], vhi[...], vlo[...], (0,))
+
+        across(i).wait_recv()
+        share(i).start()
+
+        def piece(p, carry):
+            k = i * Q + p
+
+            @pl.when(chained & (z > first))
+            def _():
+                onward(k).wait_recv()
+
+            @pl.when(adds & (z == first))
+            def _():
+                sbuf[rows(k, pw), :] = tbuf[rows(p, pw), :]
+
+            @pl.when(adds & (z > first))
+            def _():
+                sbuf[rows(k, pw), :] += tbuf[rows(p, pw), :]
+
+            @pl.when(chained & (z < last) & jnp.logical_not(source))
+            def _():
+                onward(k).start()
+            return carry
+        lax.fori_loop(0, Q, piece, 0)
+
+        share(i).wait_recv()
+
+        @pl.when(relay)
+        def _():
+            hand(i).start()
+
+        @pl.when((x == 0) & chained)
+        def _():
+            @pl.when(diag)
+            def _():
+                high, low = split(0.5 * vall[rows(i, w), pl.ds(0, half)])
+                rhi[...] = high
+                rlo[...] = low
+
+            @pl.when(jnp.logical_not(diag))
+            def _():
+                high, low = split(sbuf[rows(i, w), :])
+                rhi[...] = high
+                rlo[...] = low
+            multiply(pl.ds(0, half))
+
+        @pl.when(diag | pair)
+        def _():
+            @pl.when(diag)
+            def _():
+                high, low = split(0.5 * vall[rows(i, w), pl.ds(half, half)])
+                rhi[...] = high
+                rlo[...] = low
+
+            @pl.when(pair)
+            def _():
+                hand(i).wait_recv()
+                high, low = split(ubuf[rows(i, w), :])
+                rhi[...] = high
+                rlo[...] = low
+            multiply(pl.ds(half, half))
+        return carry
+
+    lax.fori_loop(0, steps, step, 0)
+
+    @pl.when((x == 1) & diag)
+    def _():
+        def place(t, carry):
+            img[rows(t, w), pl.ds(0, half)] = sbuf[rows(t, w), :]
+            return carry
+        lax.fori_loop(0, steps, place, 0)
+
+    mate().wait_send()
+
+    def drain(i, carry):
+        across(i).wait_send()
+        share(i).wait_send()
+
+        @pl.when(relay)
+        def _():
+            hand(i).wait_send()
+        return carry
+
+    lax.fori_loop(0, steps, drain, 0)
+
+    def sent(k, carry):
+        @pl.when(source)
+        def _():
+            origin(k).wait_send()
+
+        @pl.when(chained & (z < last) & jnp.logical_not(source))
+        def _():
+            onward(k).wait_send()
+        return carry
+
+    lax.fori_loop(0, steps * Q, sent, 0)
+
+
+def image(v, a, R, S):
+    m, kd = v.shape
+    w = kd
+    steps = m // w
+    Q = 4
+    half = S * kd
+    dma = pltpu.SemaphoreType.DMA
+    f32, bf16 = jnp.float32, jnp.bfloat16
+    return pl.pallas_call(
+        functools.partial(image_kernel, R, S, Q),
+        out_shape=(jax.ShapeDtypeStruct((m, 2 * half), f32), jax.ShapeDtypeStruct((m, 2 * half), f32)),
+        in_specs=[pl.BlockSpec(memory_space=pltpu.VMEM), pl.BlockSpec(memory_space=pl.ANY)],
+        out_specs=(pl.BlockSpec(memory_space=pltpu.VMEM), pl.BlockSpec(memory_space=pltpu.VMEM)),
+        scratch_shapes=[
+            pltpu.VMEM((m, half), f32), pltpu.VMEM((m, half), f32), pltpu.VMEM((w, half), f32),
+            pltpu.VMEM((2, m, w), f32), pltpu.VMEM((m, w), bf16), pltpu.VMEM((m, w), bf16),
+            pltpu.VMEM((m, half), bf16), pltpu.VMEM((m, half), bf16),
+            pltpu.VMEM((w, half), bf16), pltpu.VMEM((w, half), bf16),
+            dma, dma((2,)), dma, dma, dma((steps,)), dma((steps,)), dma((steps,)), dma((steps,)),
+            dma((steps,)), dma((steps,)), dma((steps * Q,)), dma((steps * Q,)),
+        ],
+        compiler_params=pltpu.CompilerParams(
+            collective_id=3, has_side_effects=True, vmem_limit_bytes=60_000_000),
+        cost_estimate=pl.CostEstimate(flops=0, bytes_accessed=100_000_000, transcendentals=0),
+        name="image",
+    )(v, a)
+
+
+def partial_general(matrix, basis_vectors):
     R = lax.axis_size("row")
     S = lax.axis_size("sub")
     C = lax.axis_size("col") * S
@@ -267,7 +541,7 @@
         part = part.reshape(per, R, piece, width).transpose(1, 0, 2, 3).reshape(R * per * piece, width)
         images.append(lax.psum_scatter(part, "row", scatter_dimension=0, tiled=True))
     mine = regroup(spread, C // S, S).reshape(per * piece, K)
-    partial_proj = jnp.concatenate(
+    return jnp.concatenate(
         [
             lax.dot_general(
                 mine,
@@ -280,7 +554,27 @@
         ],
         axis=1,
     )
-    child_block = project(partial_proj, R, C // S, S)
+
+
+def partial_halves(matrix, basis_vectors, R, S):
+    vectors, images = image(basis_vectors, matrix, R, S)
+    part = lax.dot_general(
+        vectors, images, (((0,), (0,)), ((), ())),
+        precision=lax.Precision.HIGH, preferred_element_type=jnp.float32)
+    return part + part.T
+
+
+def shards(matrix, basis_vectors, split_size):
+    R = lax.axis_size("row")
+    X = lax.axis_size("col")
+    S = lax.axis_size("sub")
+    m, n = matrix.shape
+    halves = m == n and R == X * S and X == 2 and S == 2
+    if halves:
+        partial_proj = partial_halves(matrix, basis_vectors, R, S)
+    else:
+        partial_proj = partial_general(matrix, basis_vectors)
+    child_block = project(partial_proj, R, X, S, halves)
     row_ids = (
         jnp.arange(child_block.shape[0], dtype=jnp.int32)
         + lax.axis_index("row") * child_block.shape[0]

time: 299 us -> 202 us (0.68)
  the two profiles are of different devices: /device:TPU:3 before, /device:TPU:0 now
where the time goes in v1:
time: 202 us; the launch traced here: 201 us
  Pallas kernels  167 us (83%)
  matrix products  19.4 us (10%)
  other arithmetic  8.77 us (4%)
  local copies, waits for them, and re-layouts  5.34 us (3%)
    pallas_call x1, Pallas kernels, image(): pl.pallas_call(functools.partial(image_kernel, R, S, Q), out_shape=(jax.S...  100 us
    pallas_call x1, Pallas kernels, project(): pl.pallas_call(functools.partial(project_kernel, R, X, S, relative), out_...  66.7 us
    dot_general x1, matrix products, partial_halves(): lax.dot_general(vectors, images, (((0,), (0,)), ((), ())), precision=lax....  19.4 us
    add x1, other arithmetic, partial_halves(): return part + part.T  6.76 us
    dot_general x1, local copies, waits for them, and re-layouts, partial_halves(): lax.dot_general(vectors, images, (((0,), (0,)), ((), ())), precision=lax....  5.34 us

profile of v1, /device:TPU:0, one launch (start us, length us, event | category | flops | bytes accessed | tf_op | source)
XLA Modules:
  0.0 201.3 jit_solution(5526126672446019243)
XLA Ops:
  0.0 100.4 %image.1 = (f32[2048,1024]{1,0:T(8,128)}, f32[2048,1024]{1,0:T(8,128)}) custom-call(f32[2048,256]{1,0:T(8,128)} %v.1, f32[2048,2048]{1,0:T(8,128)} %a.1), custom_call_target="tpu_custom_call" | custom-call | bytes 100000000 | tf_op jit(solution)/shard_map/image/pallas_call | solution.py:499
  100.4 19.4 %fusion.2 = f32[1024,1024]{1,0:T(8,128)} fusion(f32[2048,1024]{1,0:T(8,128)} %get-tuple-element.7, f32[2048,1024]{1,0:T(8,128)} %get-tuple-element.8), kind=kOutput, calls=%fused_computation.6 | convolution fusion | flops 12884901888 | bytes 20971520 | tf_op jit(solution)/shard_map/dot_general | solution.py:561
  119.9 5.3 %copy.4 = f32[1024,1024]{0,1:T(8,128)} copy(f32[1024,1024]{1,0:T(8,128)} %fusion.2) | data formatting | bytes 8388608 | tf_op jit(solution)/shard_map/dot_general | solution.py:561
  125.2 6.8 %bitcast_add_fusion.p = f32[1024,1024]{1,0:T(8,128)} fusion(f32[1024,1024]{1,0:T(8,128)} %fusion.2, f32[1024,1024]{0,1:T(8,128)} %copy.4), kind=kLoop, calls=%fused_computation | loop fusion | flops 1048576 | bytes 12582912 | tf_op jit(solution)/shard_map/add | solution.py:564
  132.0 66.7 %project.1 = f32[256,512]{1,0:T(8,128)} custom-call(f32[1024,1024]{1,0:T(8,128)} %bitcast_add_fusion.p), custom_call_target="tpu_custom_call" | custom-call | bytes 60000000 | tf_op jit(solution)/shard_map/project/pallas_call | solution.py:233
  199.3 2.0 select_bitcast_fusion
  (2 shorter events, 0.0 us)

commit v2 on v1

--- a/solution.py
+++ b/solution.py
@@ -263,8 +263,8 @@
     return one(a_high, b_high) + (one(a_high, b_low) + one(a_low, b_high))
 
 
-def image_kernel(R, S, Q, v, a, vall, img, sbuf, ubuf, tbuf, abuf, ahi, alo, vhi, vlo, rhi, rlo,
-                 lsem, asem, os, orr, xs, xr, fs, fr, hs, hr, ts, tr):
+def image_kernel(R, S, Q, v, a, out, vall, img, ybuf, sbuf, ubuf, tbuf, abuf, ahi, alo, vhi, vlo,
+                 ihi, ilo, rhi, rlo, lsem, asem, os, orr, xs, xr, fs, fr, hs, hr, ts, tr):
     z, x, s = lax.axis_index("row"), lax.axis_index("col"), lax.axis_index("sub")
     c = x * S + s
     m, kd = v.shape
@@ -357,14 +357,17 @@
             return carry
         lax.fori_loop(0, steps * Q, send, 0)
 
-    @pl.when(adds)
-    def _():
-        def prepare(i, carry):
-            high, low = split(vall[rows(i, w), pl.ds(0, half)])
-            vhi[rows(i, w), :] = high
-            vlo[rows(i, w), :] = low
-            return carry
-        lax.fori_loop(0, steps, prepare, 0)
+    def prepare(i, hh):
+        here, columns = rows(i, w), pl.ds(hh * half, half)
+        high, low = split(vall[here, columns])
+        vhi[here, columns] = high
+        vlo[here, columns] = low
+
+    def prepare_own(i, carry):
+        prepare(i, 0)
+        return carry
+
+    lax.fori_loop(0, steps, prepare_own, 0)
 
     def multiply(columns):
         def tile(t, carry):
@@ -389,7 +392,7 @@
 
         @pl.when(adds)
         def _():
-            tbuf[...] = weight * dot3(ahi[...], alo[...], vhi[...], vlo[...], (0,))
+            tbuf[...] = weight * dot3(ahi[...], alo[...], vhi[:, :half], vlo[:, :half], (0,))
 
         across(i).wait_recv()
         share(i).start()
@@ -416,6 +419,7 @@
         lax.fori_loop(0, Q, piece, 0)
 
         share(i).wait_recv()
+        prepare(i, 1)
 
         @pl.when(relay)
         def _():
@@ -461,6 +465,36 @@
             img[rows(t, w), pl.ds(0, half)] = sbuf[rows(t, w), :]
             return carry
         lax.fori_loop(0, steps, place, 0)
+
+    def fold(hh, present):
+        columns = pl.ds(hh * half, half)
+
+        @pl.when(present)
+        def _():
+            def halve(t, carry):
+                high, low = split(img[rows(t, w), columns])
+                ihi[rows(t, w), :] = high
+                ilo[rows(t, w), :] = low
+                return carry
+            lax.fori_loop(0, steps, halve, 0)
+            for b in range(2 * S):
+                part = slice(b * kd, (b + 1) * kd)
+                ybuf[part, columns] = dot3(vhi[:, part], vlo[:, part], ihi[...], ilo[...], (0,))
+
+        @pl.when(jnp.logical_not(present))
+        def _():
+            ybuf[:, columns] = jnp.zeros((2 * half, half), jnp.float32)
+
+    fold(1, diag | pair)
+    fold(0, chained & ((x == 0) | diag))
+    for b in range(2 * S):
+        mine = slice(b * kd, (b + 1) * kd)
+        for e in range(b, 2 * S):
+            theirs = slice(e * kd, (e + 1) * kd)
+            total = ybuf[mine, theirs] + ybuf[theirs, mine].T
+            out[mine, theirs] = total
+            if e > b:
+                out[theirs, mine] = total.T
 
     mate().wait_send()
 
@@ -498,12 +532,15 @@
     f32, bf16 = jnp.float32, jnp.bfloat16
     return pl.pallas_call(
         functools.partial(image_kernel, R, S, Q),
-        out_shape=(jax.ShapeDtypeStruct((m, 2 * half), f32), jax.ShapeDtypeStruct((m, 2 * half), f32)),
+        out_shape=jax.ShapeDtypeStruct((2 * half, 2 * half), f32),
         in_specs=[pl.BlockSpec(memory_space=pltpu.VMEM), pl.BlockSpec(memory_space=pl.ANY)],
-        out_specs=(pl.BlockSpec(memory_space=pltpu.VMEM), pl.BlockSpec(memory_space=pltpu.VMEM)),
+        out_specs=pl.BlockSpec(memory_space=pltpu.VMEM),
         scratch_shapes=[
+            pltpu.VMEM((m, 2 * half), f32), pltpu.VMEM((m, 2 * half), f32),
+            pltpu.VMEM((2 * half, 2 * half), f32),
             pltpu.VMEM((m, half), f32), pltpu.VMEM((m, half), f32), pltpu.VMEM((w, half), f32),
             pltpu.VMEM((2, m, w), f32), pltpu.VMEM((m, w), bf16), pltpu.VMEM((m, w), bf16),
+            pltpu.VMEM((m, 2 * half), bf16), pltpu.VMEM((m, 2 * half), bf16),
             pltpu.VMEM((m, half), bf16), pltpu.VMEM((m, half), bf16),
             pltpu.VMEM((w, half), bf16), pltpu.VMEM((w, half), bf16),
             dma, dma((2,)), dma, dma, dma((steps,)), dma((steps,)), dma((steps,)), dma((steps,)),
@@ -556,14 +593,6 @@
     )
 
 
-def partial_halves(matrix, basis_vectors, R, S):
-    vectors, images = image(basis_vectors, matrix, R, S)
-    part = lax.dot_general(
-        vectors, images, (((0,), (0,)), ((), ())),
-        precision=lax.Precision.HIGH, preferred_element_type=jnp.float32)
-    return part + part.T
-
-
 def shards(matrix, basis_vectors, split_size):
     R = lax.axis_size("row")
     X = lax.axis_size("col")
@@ -571,7 +600,7 @@
     m, n = matrix.shape
     halves = m == n and R == X * S and X == 2 and S == 2
     if halves:
-        partial_proj = partial_halves(matrix, basis_vectors, R, S)
+        partial_proj = image(basis_vectors, matrix, R, S)
     else:
         partial_proj = partial_general(matrix, basis_vectors)
     child_block = project(partial_proj, R, X, S, halves)

time: 202 us -> 181 us (0.90)
  the two profiles are of different devices: /device:TPU:0 before, /device:TPU:9 now
where the time goes in v2:
time: 181 us; the launch traced here: 180 us
  Pallas kernels  178 us (98%)
  other arithmetic  2.02 us (1%)
    pallas_call x1, Pallas kernels, image(): pl.pallas_call(functools.partial(image_kernel, R, S, Q), out_shape=jax.Sh...  124 us
    pallas_call x1, Pallas kernels, project(): pl.pallas_call(functools.partial(project_kernel, R, X, S, relative), out_...  53.7 us

profile of v2, /device:TPU:9, one launch (start us, length us, event | category | flops | bytes accessed | tf_op | source)
XLA Modules:
  0.0 180.4 jit_solution(12835715139843559786)
XLA Ops:
  0.0 124.0 %image.1.p = f32[1024,1024]{1,0:T(8,128)} custom-call(f32[2048,256]{1,0:T(8,128)} %v.1, f32[2048,2048]{1,0:T(8,128)} %a.1), custom_call_target="tpu_custom_call" | custom-call | bytes 100000000 | tf_op jit(solution)/shard_map/image/pallas_call | solution.py:533
  124.0 53.7 %project.1 = f32[256,512]{1,0:T(8,128)} custom-call(f32[1024,1024]{1,0:T(8,128)} %image.1.p), custom_call_target="tpu_custom_call" | custom-call | bytes 60000000 | tf_op jit(solution)/shard_map/project/pallas_call | solution.py:233
  178.4 2.0 %select_bitcast_fusion = f32[1,256,512]{2,1,0:T(8,128)} fusion(f32[256,512]{1,0:T(8,128)} %project.1, pred[512]{0:T(512)(128)(4,1)S(1)} %get-tuple-element.7, pred[512]{0:T(512)(128)(4,1)S(1)} %get-tuple-element.8, pred[]{:T(512)S(6)} %eq.3, pred[256]{0:T(512)(128)(4,1)S(1)} %get-tuple-element.5, pred[256]{0:T(512)(128)(4,1)S(1)} %get-tuple-element.6), kind=kLoop, calls=%fused_computation | loop fusion | flops 524288 | bytes 1050113 | tf_op jit(solution)/shard_map/broadcast_in_dim | solution.py:621
  (2 shorter events, 0.0 us)

commit v3 on v2

--- a/solution.py
+++ b/solution.py
@@ -338,6 +338,7 @@
     own.start()
     load(0).start()
     img[...] = jnp.zeros_like(img)
+    ybuf[...] = jnp.zeros_like(ybuf)
     pl.semaphore_wait(barrier, 2 + S * ((z > 0).astype(jnp.int32) + (z < R - 1).astype(jnp.int32)))
     mate().start()
 
@@ -376,7 +377,12 @@
             return carry
         lax.fori_loop(0, steps, tile, 0)
 
-    def step(i, carry):
+    def feed(value):
+        high, low = split(value)
+        rhi[...] = high
+        rlo[...] = low
+
+    def open_block(i):
         load(i).wait()
 
         @pl.when(i < steps - 1)
@@ -390,12 +396,55 @@
             return carry
         lax.fori_loop(0, steps, cut, 0)
 
-        @pl.when(adds)
-        def _():
-            tbuf[...] = weight * dot3(ahi[...], alo[...], vhi[:, :half], vlo[:, :half], (0,))
-
+    def receive(i):
         across(i).wait_recv()
         share(i).start()
+
+    def collect(i):
+        share(i).wait_recv()
+        prepare(i, 1)
+
+        @pl.when(relay)
+        def _():
+            hand(i).start()
+
+    def fold(hh):
+        columns = pl.ds(hh * half, half)
+
+        def halve(t, carry):
+            high, low = split(img[rows(t, w), columns])
+            ihi[rows(t, w), :] = high
+            ilo[rows(t, w), :] = low
+            return carry
+        lax.fori_loop(0, steps, halve, 0)
+        for b in range(2 * S):
+            part = slice(b * kd, (b + 1) * kd)
+            ybuf[part, columns] = dot3(vhi[:, part], vlo[:, part], ihi[...], ilo[...], (0,))
+
+    def local_step(i, carry):
+        receive(i)
+        open_block(i)
+
+        @pl.when(x == 0)
+        def _():
+            feed(0.5 * vall[rows(i, w), pl.ds(0, half)])
+            multiply(pl.ds(0, half))
+        collect(i)
+        feed(0.5 * vall[rows(i, w), pl.ds(half, half)])
+        multiply(pl.ds(half, half))
+        return carry
+
+    def stream_step(i, carry):
+        @pl.when(jnp.logical_not(diag) & (2 * i < steps))
+        def _():
+            receive(2 * i)
+            receive(2 * i + 1)
+
+        open_block(i)
+
+        @pl.when(adds)
+        def _():
+            tbuf[...] = weight * dot3(ahi[...], alo[...], vhi[:, :half], vlo[:, :half], (0,))
 
         def piece(p, carry):
             k = i * Q + p
@@ -412,81 +461,63 @@
             def _():
                 sbuf[rows(k, pw), :] += tbuf[rows(p, pw), :]
 
-            @pl.when(chained & (z < last) & jnp.logical_not(source))
+            @pl.when(chained & (z < last))
             def _():
                 onward(k).start()
             return carry
         lax.fori_loop(0, Q, piece, 0)
 
-        share(i).wait_recv()
-        prepare(i, 1)
-
-        @pl.when(relay)
-        def _():
-            hand(i).start()
+        lag = jnp.where(relay, 0, steps // 2)
+
+        @pl.when(jnp.logical_not(diag) & (i >= lag) & (2 * (i - lag) < steps))
+        def _():
+            collect(2 * (i - lag))
+            collect(2 * (i - lag) + 1)
 
         @pl.when((x == 0) & chained)
         def _():
-            @pl.when(diag)
-            def _():
-                high, low = split(0.5 * vall[rows(i, w), pl.ds(0, half)])
-                rhi[...] = high
-                rlo[...] = low
-
-            @pl.when(jnp.logical_not(diag))
-            def _():
-                high, low = split(sbuf[rows(i, w), :])
-                rhi[...] = high
-                rlo[...] = low
+            feed(sbuf[rows(i, w), :])
             multiply(pl.ds(0, half))
 
-        @pl.when(diag | pair)
-        def _():
-            @pl.when(diag)
-            def _():
-                high, low = split(0.5 * vall[rows(i, w), pl.ds(half, half)])
-                rhi[...] = high
-                rlo[...] = low
-
-            @pl.when(pair)
-            def _():
-                hand(i).wait_recv()
-                high, low = split(ubuf[rows(i, w), :])
-                rhi[...] = high
-                rlo[...] = low
+        @pl.when((x == 1) & diag)
+        def _():
+            feed(sbuf[rows(i, w), :])
+            for b in range(2 * S):
+                part = slice(b * kd, (b + 1) * kd)
+                ybuf[part, :half] += dot3(vhi[rows(i, w), part], vlo[rows(i, w), part], rhi[...], rlo[...], (0,))
+
+        @pl.when(pair)
+        def _():
+            hand(i).wait_recv()
+            feed(ubuf[rows(i, w), :])
             multiply(pl.ds(half, half))
         return carry
 
-    lax.fori_loop(0, steps, step, 0)
-
-    @pl.when((x == 1) & diag)
+    @pl.when(diag)
     def _():
-        def place(t, carry):
-            img[rows(t, w), pl.ds(0, half)] = sbuf[rows(t, w), :]
-            return carry
-        lax.fori_loop(0, steps, place, 0)
-
-    def fold(hh, present):
-        columns = pl.ds(hh * half, half)
-
-        @pl.when(present)
-        def _():
-            def halve(t, carry):
-                high, low = split(img[rows(t, w), columns])
-                ihi[rows(t, w), :] = high
-                ilo[rows(t, w), :] = low
-                return carry
-            lax.fori_loop(0, steps, halve, 0)
-            for b in range(2 * S):
-                part = slice(b * kd, (b + 1) * kd)
-                ybuf[part, columns] = dot3(vhi[:, part], vlo[:, part], ihi[...], ilo[...], (0,))
-
-        @pl.when(jnp.logical_not(present))
-        def _():
-            ybuf[:, columns] = jnp.zeros((2 * half, half), jnp.float32)
-
-    fold(1, diag | pair)
-    fold(0, chained & ((x == 0) | diag))
+        lax.fori_loop(0, steps, local_step, 0)
+        fold(1)
+
+        @pl.when(x == 0)
+        def _():
+            fold(0)
+
+        @pl.when(x == 1)
+        def _():
+            load(0).start()
+
+    @pl.when(jnp.logical_not(source))
+    def _():
+        lax.fori_loop(0, steps, stream_step, 0)
+
+    @pl.when(pair)
+    def _():
+        fold(1)
+
+    @pl.when((x == 0) & chained & jnp.logical_not(diag))
+    def _():
+        fold(0)
+
     for b in range(2 * S):
         mine = slice(b * kd, (b + 1) * kd)
         for e in range(b, 2 * S):

time: 181 us -> 172 us (0.950)
  the two profiles are of different devices: /device:TPU:9 before, /device:TPU:3 now
where the time goes in v3:
time: 172 us; the launch traced here: 170 us
  Pallas kernels  167 us (97%)
  other arithmetic  2.02 us (1%)
    pallas_call x1, Pallas kernels, image(): pl.pallas_call(functools.partial(image_kernel, R, S, Q), out_shape=jax.Sh...  110 us
    pallas_call x1, Pallas kernels, project(): pl.pallas_call(functools.partial(project_kernel, R, X, S, relative), out_...  57.1 us

profile of v3, /device:TPU:3, one launch (start us, length us, event | category | flops | bytes accessed | tf_op | source)
XLA Modules:
  0.0 169.8 jit_solution(1797979924910957947)
XLA Ops:
  0.0 110.0 %image.1.p = f32[1024,1024]{1,0:T(8,128)} custom-call(f32[2048,256]{1,0:T(8,128)} %v.1, f32[2048,2048]{1,0:T(8,128)} %a.1), custom_call_target="tpu_custom_call" | custom-call | bytes 100000000 | tf_op jit(solution)/shard_map/image/pallas_call | solution.py:564
  110.0 57.1 %project.1 = f32[256,512]{1,0:T(8,128)} custom-call(f32[1024,1024]{1,0:T(8,128)} %image.1.p), custom_call_target="tpu_custom_call" | custom-call | bytes 60000000 | tf_op jit(solution)/shard_map/project/pallas_call | solution.py:233
  167.8 2.0 %select_bitcast_fusion = f32[1,256,512]{2,1,0:T(8,128)} fusion(f32[256,512]{1,0:T(8,128)} %project.1, pred[512]{0:T(512)(128)(4,1)S(1)} %get-tuple-element.7, pred[512]{0:T(512)(128)(4,1)S(1)} %get-tuple-element.8, pred[]{:T(512)S(6)} %eq.3, pred[256]{0:T(512)(128)(4,1)S(1)} %get-tuple-element.5, pred[256]{0:T(512)(128)(4,1)S(1)} %get-tuple-element.6), kind=kLoop, calls=%fused_computation | loop fusion | flops 524288 | bytes 1050113 | tf_op jit(solution)/shard_map/broadcast_in_dim | solution.py:652
  (2 shorter events, 0.0 us)

commit v4 on v3

--- a/solution.py
+++ b/solution.py
@@ -263,8 +263,9 @@
     return one(a_high, b_high) + (one(a_high, b_low) + one(a_low, b_high))
 
 
-def image_kernel(R, S, Q, v, a, out, vall, img, ybuf, sbuf, ubuf, tbuf, abuf, ahi, alo, vhi, vlo,
-                 ihi, ilo, rhi, rlo, lsem, asem, os, orr, xs, xr, fs, fr, hs, hr, ts, tr):
+def image_kernel(R, S, Q, J, v, a, out, vall, img, ybuf, sbuf, ubuf, tbuf, abuf, ahi, alo, vhi, vlo,
+                 ihi, ilo, rhi, rlo, side, dbuf, lsem, asem, os, orr, xs, xr, fs, fr, hs, hr, ts, tr,
+                 ds, dr):
     z, x, s = lax.axis_index("row"), lax.axis_index("col"), lax.axis_index("sub")
     c = x * S + s
     m, kd = v.shape
@@ -279,6 +280,11 @@
     pair = (z == x * S + 1) & (s == 0)
     relay = (z == x * S) & (s == 1 - x)
     adds = (x == 1) & chained
+    cut = steps - J
+    below = jnp.logical_not(diag) & jnp.where(x == 0, z > c, z < c)
+    whole = diag | (below & (z // S == x))
+    tiles = jnp.where(whole, steps, cut)
+    count = jnp.where(x == 0, cut, steps)
     weight = jnp.where(diag, 0.5, 1.0).astype(jnp.float32)
     other = 1 - s
 
@@ -302,8 +308,12 @@
         for t in range(S):
             pl.semaphore_signal(barrier, inc=1, device_id={"row": z + 1, "sub": t}, device_id_type=MESH)
 
-    def load(i):
-        return pltpu.make_async_copy(a.at[:, rows(i, w)], abuf.at[lax.rem(i, 2)], asem.at[lax.rem(i, 2)])
+    def load(i, slot=None):
+        slot = lax.rem(i, 2) if slot is None else slot
+        return pltpu.make_async_copy(a.at[:, rows(i, w)], abuf.at[slot], asem.at[slot])
+
+    def chunk(n):
+        return lax.rem(n + cut, steps)
 
     def mate():
         return pltpu.make_async_remote_copy(
@@ -334,29 +344,56 @@
             sbuf.at[rows(k, pw), :], sbuf.at[rows(k, pw), :], ts.at[k], tr.at[k],
             device_id={"row": z + 1}, device_id_type=MESH)
 
+    def fall(k):
+        g, p = k // Q, lax.rem(k, Q)
+        return pltpu.make_async_remote_copy(
+            side.at[g, rows(p, pw), :], dbuf.at[rows(k, pw), :], ds.at[k], dr.at[k],
+            device_id={"row": z - 1}, device_id_type=MESH)
+
+    def drop(k, hh):
+        base = lax.rem(k, J * Q) + cut * Q
+        return pltpu.make_async_remote_copy(
+            vall.at[rows(base, pw), pl.ds(hh * half, half)], dbuf.at[rows(k, pw), :], ds.at[k], dr.at[k],
+            device_id={"row": z - 1}, device_id_type=MESH)
+
+    def pass_down(k):
+        return pltpu.make_async_remote_copy(
+            dbuf.at[rows(k, pw), :], dbuf.at[rows(k, pw), :], ds.at[k], dr.at[k],
+            device_id={"row": z - 1}, device_id_type=MESH)
+
+    def each(lo, hi, act):
+        def go(k, carry):
+            act(k)
+            return carry
+        lax.fori_loop(lo, hi, go, 0)
+
     own = pltpu.make_async_copy(v, vall.at[:, block(0, s)], lsem)
     own.start()
-    load(0).start()
+
+    @pl.when(diag)
+    def _():
+        load(chunk(0)).start()
+
+    @pl.when(jnp.logical_not(diag))
+    def _():
+        load(0).start()
     img[...] = jnp.zeros_like(img)
     ybuf[...] = jnp.zeros_like(ybuf)
     pl.semaphore_wait(barrier, 2 + S * ((z > 0).astype(jnp.int32) + (z < R - 1).astype(jnp.int32)))
     mate().start()
 
-    def begin(i, carry):
-        across(i).start()
-        return carry
-
-    lax.fori_loop(0, steps, begin, 0)
+    each(0, steps, lambda n: across(chunk(n)).start())
     own.wait()
     mate().wait_recv()
     source = (x == 0) & diag
 
     @pl.when(source)
     def _():
-        def send(k, carry):
-            origin(k).start()
-            return carry
-        lax.fori_loop(0, steps * Q, send, 0)
+        each(0, cut * Q, lambda k: origin(k).start())
+
+    @pl.when((x == 1) & diag)
+    def _():
+        each(0, J * Q, lambda k: drop(k, 0).start())
 
     def prepare(i, hh):
         here, columns = rows(i, w), pl.ds(hh * half, half)
@@ -375,26 +412,66 @@
             here = rows(t, w)
             img[here, columns] += dot3(ahi[here, :], alo[here, :], rhi[...], rlo[...], (1,))
             return carry
-        lax.fori_loop(0, steps, tile, 0)
+        lax.fori_loop(0, tiles, tile, 0)
 
     def feed(value):
         high, low = split(value)
         rhi[...] = high
         rlo[...] = low
 
-    def open_block(i):
-        load(i).wait()
-
-        @pl.when(i < steps - 1)
-        def _():
-            load(i + 1).start()
-
-        def cut(t, carry):
-            high, low = split(abuf[lax.rem(i, 2), rows(t, w), :])
+    def slice_block(slot):
+        def piece(t):
+            high, low = split(abuf[slot, rows(t, w), :])
             ahi[rows(t, w), :] = high
             alo[rows(t, w), :] = low
-            return carry
-        lax.fori_loop(0, steps, cut, 0)
+        each(0, steps, piece)
+
+    def open_block(i, until):
+        load(i).wait()
+
+        @pl.when(i < until - 1)
+        def _():
+            load(i + 1).start()
+        slice_block(lax.rem(i, 2))
+
+    def sides(hh, slot):
+        columns = slice(hh * half, (hh + 1) * half)
+
+        def act(j):
+            load(cut + j, slot).start()
+            load(cut + j, slot).wait()
+            slice_block(slot)
+            g = hh * J + j
+            side[g] = dot3(ahi[...], alo[...], vhi[:, columns], vlo[:, columns], (0,))
+
+            @pl.when(z == R - 1)
+            def _():
+                each(g * Q, (g + 1) * Q, lambda k: fall(k).start())
+        each(0, J, act)
+
+    def descend(g):
+        def act(k):
+            pass_down(k).wait_recv()
+
+            @pl.when(x == 0)
+            def _():
+                side[g, rows(lax.rem(k, Q), pw), :] += dbuf[rows(k, pw), :]
+                fall(k).start()
+
+            @pl.when(x == 1)
+            def _():
+                pass_down(k).start()
+        each(g * Q, (g + 1) * Q, act)
+
+    def gather_fold(g_rows, hh, i):
+        feed(g_rows)
+        columns = rows(hh, half)
+
+        def act(b):
+            part = rows(b, kd)
+            ybuf[part, columns] += dot3(
+                vhi[rows(i, w), part], vlo[rows(i, w), part], rhi[...], rlo[...], (0,))
+        each(0, 2 * S, act)
 
     def receive(i):
         across(i).wait_recv()
@@ -404,9 +481,14 @@
         share(i).wait_recv()
         prepare(i, 1)
 
-        @pl.when(relay)
+        @pl.when(relay & (i < jnp.where(x == 0, cut, steps)))
         def _():
             hand(i).start()
+
+        @pl.when((x == 1) & diag & (i >= cut))
+        def _():
+            base = (i - cut + J) * Q
+            each(base, base + Q, lambda k: drop(k, 1).start())
 
     def fold(hh):
         columns = pl.ds(hh * half, half)
@@ -417,13 +499,27 @@
             ilo[rows(t, w), :] = low
             return carry
         lax.fori_loop(0, steps, halve, 0)
-        for b in range(2 * S):
-            part = slice(b * kd, (b + 1) * kd)
+        def act(b):
+            part = rows(b, kd)
             ybuf[part, columns] = dot3(vhi[:, part], vlo[:, part], ihi[...], ilo[...], (0,))
-
-    def local_step(i, carry):
-        receive(i)
-        open_block(i)
+        each(0, 2 * S, act)
+
+    def local_step(n, carry):
+        i = chunk(n)
+
+        @pl.when(n == 0)
+        def _():
+            receive(i)
+
+        @pl.when(n < steps - 1)
+        def _():
+            receive(chunk(n + 1))
+        load(i).wait()
+
+        @pl.when(n < steps - 1)
+        def _():
+            load(chunk(n + 1)).start()
+        slice_block(lax.rem(i, 2))
 
         @pl.when(x == 0)
         def _():
@@ -437,16 +533,27 @@
     def stream_step(i, carry):
         @pl.when(jnp.logical_not(diag) & (2 * i < steps))
         def _():
-            receive(2 * i)
-            receive(2 * i + 1)
-
-        open_block(i)
-
-        @pl.when(adds)
+            receive(chunk(2 * i))
+            receive(chunk(2 * i + 1))
+
+        turn = jnp.where(z == R - 1, steps // 2 - 1, steps // 2)
+
+        @pl.when((x == 0) & below & (i == turn))
+        def _():
+            each(0, steps, lambda n: collect(chunk(n)))
+            sides(1, lax.rem(i + 1, 2))
+
+        open_block(i, count)
+
+        @pl.when(adds & whole)
         def _():
             tbuf[...] = weight * dot3(ahi[...], alo[...], vhi[:, :half], vlo[:, :half], (0,))
 
-        def piece(p, carry):
+        @pl.when(adds & jnp.logical_not(whole) & (i < cut))
+        def _():
+            tbuf[...] = dot3(ahi[:cut * w, :], alo[:cut * w, :], vhi[:cut * w, :half], vlo[:cut * w, :half], (0,))
+
+        def piece(p):
             k = i * Q + p
 
             @pl.when(chained & (z > first))
@@ -464,27 +571,54 @@
             @pl.when(chained & (z < last))
             def _():
                 onward(k).start()
-            return carry
-        lax.fori_loop(0, Q, piece, 0)
+
+        @pl.when(i < cut)
+        def _():
+            each(0, Q, piece)
+
+        @pl.when((x == 1) & diag & (i >= cut))
+        def _():
+            sbuf[rows(i, w), :] = tbuf[...]
+
+        for g in range(2 * J):
+            due_up = (x == 0) & (z < R - 1) & (i == (g + R - z if g < J else cut - 1))
+            if g > J:
+                due_up = jnp.bool_(False)
+            elif g == J:
+                due_up = due_up & (z == R - 2)
+            due = due_up | ((x == 1) & (z > 0) & (i == g + c - z))
+
+            @pl.when(below & due)
+            def _():
+                descend(g)
 
         lag = jnp.where(relay, 0, steps // 2)
 
-        @pl.when(jnp.logical_not(diag) & (i >= lag) & (2 * (i - lag) < steps))
-        def _():
-            collect(2 * (i - lag))
-            collect(2 * (i - lag) + 1)
-
-        @pl.when((x == 0) & chained)
+        @pl.when(jnp.logical_not(diag) & ((x == 1) | relay) & (i >= lag) & (2 * (i - lag) < steps))
+        def _():
+            collect(chunk(2 * (i - lag)))
+            collect(chunk(2 * (i - lag) + 1))
+
+        @pl.when((x == 0) & below)
         def _():
             feed(sbuf[rows(i, w), :])
             multiply(pl.ds(0, half))
 
         @pl.when((x == 1) & diag)
         def _():
-            feed(sbuf[rows(i, w), :])
-            for b in range(2 * S):
-                part = slice(b * kd, (b + 1) * kd)
-                ybuf[part, :half] += dot3(vhi[rows(i, w), part], vlo[rows(i, w), part], rhi[...], rlo[...], (0,))
+            gather_fold(sbuf[rows(i, w), :], 0, i)
+
+        @pl.when((x == 1) & below & (i >= cut))
+        def _():
+            j = i - cut
+            for hh in range(2):
+                g = hh * J + j
+
+                @pl.when(z == 0)
+                def _():
+                    each(g * Q, (g + 1) * Q, lambda k: pass_down(k).wait_recv())
+                feed(dbuf[rows(g, w), :])
+                multiply(pl.ds(hh * half, half))
 
         @pl.when(pair)
         def _():
@@ -493,6 +627,10 @@
             multiply(pl.ds(half, half))
         return carry
 
+    @pl.when((x == 0) & below)
+    def _():
+        sides(0, 1)
+
     @pl.when(diag)
     def _():
         lax.fori_loop(0, steps, local_step, 0)
@@ -501,6 +639,10 @@
         @pl.when(x == 0)
         def _():
             fold(0)
+            def absorb(g):
+                each(g * Q, (g + 1) * Q, lambda k: pass_down(k).wait_recv())
+                gather_fold(dbuf[rows(g, w), :], g // J, cut + lax.rem(g, J))
+            each(0, 2 * J, absorb)
 
         @pl.when(x == 1)
         def _():
@@ -508,13 +650,21 @@
 
     @pl.when(jnp.logical_not(source))
     def _():
-        lax.fori_loop(0, steps, stream_step, 0)
-
-    @pl.when(pair)
+        lax.fori_loop(0, count, stream_step, 0)
+
+    @pl.when((x == 0) & below & (z < R - 1))
+    def _():
+        @pl.when(z < R - 2)
+        def _():
+            descend(J)
+        for g in range(J + 1, 2 * J):
+            descend(g)
+
+    @pl.when(pair | ((x == 1) & below))
     def _():
         fold(1)
 
-    @pl.when((x == 0) & chained & jnp.logical_not(diag))
+    @pl.when(below)
     def _():
         fold(0)
 
@@ -529,28 +679,35 @@
 
     mate().wait_send()
 
-    def drain(i, carry):
+    def drain(i):
         across(i).wait_send()
         share(i).wait_send()
 
-        @pl.when(relay)
+        @pl.when(relay & (i < jnp.where(x == 0, cut, steps)))
         def _():
             hand(i).wait_send()
-        return carry
-
-    lax.fori_loop(0, steps, drain, 0)
-
-    def sent(k, carry):
-        @pl.when(source)
-        def _():
-            origin(k).wait_send()
-
-        @pl.when(chained & (z < last) & jnp.logical_not(source))
-        def _():
-            onward(k).wait_send()
-        return carry
-
-    lax.fori_loop(0, steps * Q, sent, 0)
+    each(0, steps, drain)
+
+    @pl.when(source)
+    def _():
+        each(0, cut * Q, lambda k: origin(k).wait_send())
+
+    @pl.when(chained & (z < last) & jnp.logical_not(source))
+    def _():
+        each(0, cut * Q, lambda k: onward(k).wait_send())
+
+    @pl.when((x == 0) & below)
+    def _():
+        each(0, 2 * J * Q, lambda k: fall(k).wait_send())
+
+    @pl.when((x == 1) & diag)
+    def _():
+        each(0, J * Q, lambda k: drop(k, 0).wait_send())
+        each(J * Q, 2 * J * Q, lambda k: drop(k, 1).wait_send())
+
+    @pl.when((x == 1) & below & (z > 0))
+    def _():
+        each(0, 2 * J * Q, lambda k: pass_down(k).wait_send())
 
 
 def image(v, a, R, S):
@@ -558,11 +715,12 @@
     w = kd
     steps = m // w
     Q = 4
+    J = steps // 4
     half = S * kd
     dma = pltpu.SemaphoreType.DMA
     f32, bf16 = jnp.float32, jnp.bfloat16
     return pl.pallas_call(
-        functools.partial(image_kernel, R, S, Q),
+        functools.partial(image_kernel, R, S, Q, J),
         out_shape=jax.ShapeDtypeStruct((2 * half, 2 * half), f32),
         in_specs=[pl.BlockSpec(memory_space=pltpu.VMEM), pl.BlockSpec(memory_space=pl.ANY)],
         out_specs=pl.BlockSpec(memory_space=pltpu.VMEM),
@@ -574,11 +732,13 @@
             pltpu.VMEM((m, 2 * half), bf16), pltpu.VMEM((m, 2 * half), bf16),
             pltpu.VMEM((m, half), bf16), pltpu.VMEM((m, half), bf16),
             pltpu.VMEM((w, half), bf16), pltpu.VMEM((w, half), bf16),
+            pltpu.VMEM((2 * J, w, half), f32), pltpu.VMEM((2 * J * w, half), f32),
             dma, dma((2,)), dma, dma, dma((steps,)), dma((steps,)), dma((steps,)), dma((steps,)),
             dma((steps,)), dma((steps,)), dma((steps * Q,)), dma((steps * Q,)),
+            dma((2 * J * Q,)), dma((2 * J * Q,)),
         ],
         compiler_params=pltpu.CompilerParams(
-            collective_id=3, has_side_effects=True, vmem_limit_bytes=60_000_000),
+            collective_id=3, has_side_effects=True, vmem_limit_bytes=64_000_000),
         cost_estimate=pl.CostEstimate(flops=0, bytes_accessed=100_000_000, transcendentals=0),
         name="image",
     )(v, a)

time: 172 us -> 179 us (1.041); the launches traced: 170 us -> 179 us
  Pallas kernels: 167 us -> 176 us
    pallas_call x1, Pallas kernels: 110 us -> 116 us  [image(): pl.pallas_call(functools.partial(image_kernel, R, S, Q, J), out_shape=jax...]
    pallas_call x1, Pallas kernels: 57.1 us -> 59.5 us  [project(): pl.pallas_call(functools.partial(project_kernel, R, X, S, relative), out_...]
where the time goes in v4:
time: 179 us
  Pallas kernels  176 us (98%)
  other arithmetic  2.02 us (1%)
    pallas_call x1, Pallas kernels, image(): pl.pallas_call(functools.partial(image_kernel, R, S, Q, J), out_shape=jax...  116 us
    pallas_call x1, Pallas kernels, project(): pl.pallas_call(functools.partial(project_kernel, R, X, S, relative), out_...  59.5 us

profile of v4, /device:TPU:3, one launch (start us, length us, event | category | flops | bytes accessed | tf_op | source)
XLA Modules:
  0.0 178.6 jit_solution(7590402740370488811)
XLA Ops:
  0.0 116.4 %image.1.p = f32[1024,1024]{1,0:T(8,128)} custom-call(f32[2048,256]{1,0:T(8,128)} %v.1, f32[2048,2048]{1,0:T(8,128)} %a.1), custom_call_target="tpu_custom_call" | custom-call | bytes 100000000 | tf_op jit(solution)/shard_map/image/pallas_call | solution.py:722
  116.4 59.5 %project.1 = f32[256,512]{1,0:T(8,128)} custom-call(f32[1024,1024]{1,0:T(8,128)} %image.1.p), custom_call_target="tpu_custom_call" | custom-call | bytes 60000000 | tf_op jit(solution)/shard_map/project/pallas_call | solution.py:233
  176.6 2.0 %select_bitcast_fusion = f32[1,256,512]{2,1,0:T(8,128)} fusion(f32[256,512]{1,0:T(8,128)} %project.1, pred[512]{0:T(512)(128)(4,1)S(1)} %get-tuple-element.7, pred[512]{0:T(512)(128)(4,1)S(1)} %get-tuple-element.8, pred[]{:T(512)S(6)} %eq.3, pred[256]{0:T(512)(128)(4,1)S(1)} %get-tuple-element.5, pred[256]{0:T(512)(128)(4,1)S(1)} %get-tuple-element.6), kind=kLoop, calls=%fused_computation | loop fusion | flops 524288 | bytes 1050113 | tf_op jit(solution)/shard_map/broadcast_in_dim | solution.py:812
  (2 shorter events, 0.0 us)

commit v5 on v3

--- a/solution.py
+++ b/solution.py
@@ -132,7 +132,7 @@
     )(spread)
 
 
-def project_kernel(R, X, S, relative, p, out, acc, from_sub, from_col, from_row, res, from_pair,
+def project_kernel(R, X, S, p, out, acc, from_sub, from_col, from_row, res, from_pair,
                    a_s, a_r, b_s, b_r, c_s, c_r, d_s, d_r):
     r, x, s = lax.axis_index("row"), lax.axis_index("col"), lax.axis_index("sub")
     K = p.shape[0]
@@ -143,14 +143,6 @@
 
     def columns(cx, cs):
         return pl.ds(pl.multiple_of((cx * S + cs) * kd, kd), kd)
-
-    def held(i):
-        if not relative:
-            return rows(i)
-        return rows(lax.rem(i // S + X - x, X) * S + lax.rem(i, S))
-
-    def held_columns(d, cs):
-        return columns(d if relative else col(d), cs)
 
     def col(d):
         return lax.rem(x + d, X)
@@ -170,7 +162,7 @@
         for e in range(1, S):
             other = lax.rem(s + e, S)
             pair[d, e] = pltpu.make_async_remote_copy(
-                p.at[:, held_columns(d, other)], from_sub.at[e - 1, d],
+                p.at[:, columns(col(d), other)], from_sub.at[e - 1, d],
                 a_s.at[e - 1, d], a_r.at[e - 1, d],
                 device_id={"sub": other}, device_id_type=MESH)
             pair[d, e].start()
@@ -180,10 +172,9 @@
             pair[d, e].wait_recv()
         for q in steps:
             here = rows(lax.rem(r + q, R))
-            there = held(lax.rem(r + q, R))
-            total = p[there, held_columns(d, s)]
+            total = p[here, columns(col(d), s)]
             for e in range(1, S):
-                total = total + from_sub[e - 1, d, there, :]
+                total = total + from_sub[e - 1, d, here, :]
             acc[d, here, :] = total
             if d > 0:
                 cross[d, q] = pltpu.make_async_remote_copy(
@@ -225,13 +216,13 @@
         copy.wait_send()
 
 
-def project(partial, R, X, S, relative):
+def project(partial, R, X, S):
     K = partial.shape[0]
     rb, kd = K // R, K // (X * S)
     dma = pltpu.SemaphoreType.DMA
     f32 = jnp.float32
     return pl.pallas_call(
-        functools.partial(project_kernel, R, X, S, relative),
+        functools.partial(project_kernel, R, X, S),
         out_shape=jax.ShapeDtypeStruct((rb, S * kd), f32),
         in_specs=[pl.BlockSpec(memory_space=pltpu.VMEM)],
         out_specs=pl.BlockSpec(memory_space=pltpu.VMEM),
@@ -263,8 +254,143 @@
     return one(a_high, b_high) + (one(a_high, b_low) + one(a_low, b_high))
 
 
-def image_kernel(R, S, Q, v, a, out, vall, img, ybuf, sbuf, ubuf, tbuf, abuf, ahi, alo, vhi, vlo,
-                 ihi, ilo, rhi, rlo, lsem, asem, os, orr, xs, xr, fs, fr, hs, hr, ts, tr):
+def owners(R, S):
+    blocks, chips, columns = [], {}, {}
+    pairs = [(i, i) for i in range(R)]
+    pairs += sorted(((i, j) for i in range(R) for j in range(i + 1, R)), key=lambda p: (p[0] - p[1], p))
+    for i, j in pairs:
+        choices = [(j // S, i), (i // S, j)]
+        best = min(choices, key=lambda o: (chips.get(o, 0), columns.get(o[0], 0)))
+        slot = chips.get(best, 0)
+        chips[best] = slot + 1
+        columns[best[0]] = columns.get(best[0], 0) + 1
+        blocks.append((i, j, best[0], best[1], slot))
+    return blocks[R:] + blocks[:R], max(chips.values())
+
+
+def reduce_blocks(R, S, blocks, out, ybuf, part, r_sub, r_col, r_row, flip, tile_ref,
+                  ps, pr, qs, qr, us, ur, gs, gr, es, er):
+    z, x, s = lax.axis_index("row"), lax.axis_index("col"), lax.axis_index("sub")
+    other = 1 - s
+    kd = part.shape[1]
+    hr = kd // S
+    mine = pl.ds(pl.multiple_of(s * hr, hr), hr)
+    theirs = pl.ds(pl.multiple_of(other * hr, hr), hr)
+
+    def held(g):
+        return pl.ds(pl.multiple_of((jnp.where(x == g // S, 0, 1) * S + g % S) * kd, kd), kd)
+
+    def swap(t):
+        return pltpu.make_async_remote_copy(
+            part.at[t, theirs, :], r_sub.at[t], ps.at[t], pr.at[t],
+            device_id={"sub": other}, device_id_type=MESH)
+
+    def cross(t):
+        return pltpu.make_async_remote_copy(
+            part.at[t, mine, :], r_col.at[t], qs.at[t], qr.at[t],
+            device_id={"col": 1 - x}, device_id_type=MESH)
+
+    def along(t, sender):
+        return pltpu.make_async_remote_copy(
+            part.at[t, mine, :], r_row.at[sender, blocks[t][4]], us.at[t], ur.at[sender, blocks[t][4]],
+            device_id={"row": blocks[t][3]}, device_id_type=MESH)
+
+    def region(t, direct):
+        i, j = blocks[t][:2]
+        if direct:
+            return tile_ref.at[j % S, mine, :]
+        return tile_ref.at[i % S, :, mine]
+
+    def chip(t, direct):
+        i, j = blocks[t][:2]
+        return (j // S, i) if direct else (i // S, j)
+
+    def far(t, direct):
+        xo, zo = chip(t, direct)
+        return pltpu.make_async_remote_copy(
+            part.at[t, mine, :] if direct else flip.at[t], region(t, direct), gs.at[t], gr.at[t],
+            device_id={"col": xo, "row": zo}, device_id_type=MESH)
+
+    def near(t, direct):
+        slot = blocks[t][1] % S if direct else blocks[t][0] % S
+        return pltpu.make_async_remote_copy(
+            region(t, direct), region(t, direct), es.at[slot], er.at[slot],
+            device_id={"sub": other}, device_id_type=MESH)
+
+    for t, (i, j, xo, zo, slot) in enumerate(blocks):
+        part[t] = ybuf[held(i), held(j)] + ybuf[held(j), held(i)].T
+        swap(t).start()
+    for t, (i, j, xo, zo, slot) in enumerate(blocks):
+        swap(t).wait_recv()
+        part[t, mine, :] += r_sub[t]
+
+        @pl.when(x != xo)
+        def _():
+            cross(t).start()
+    for t, (i, j, xo, zo, slot) in enumerate(blocks):
+        @pl.when(x == xo)
+        def _():
+            cross(t).wait_recv()
+            part[t, mine, :] += r_col[t]
+
+            @pl.when(z != zo)
+            def _():
+                along(t, z).start()
+    for t, (i, j, xo, zo, slot) in enumerate(blocks):
+        straight = (xo, zo) == (j // S, i)
+
+        @pl.when((x == xo) & (z == zo))
+        def _():
+            for q in range(R):
+                if q != zo:
+                    along(t, q).wait_recv()
+                    part[t, mine, :] += r_row[q, slot]
+            value = part[t, mine, :]
+            if i != j:
+                flip[t] = value.T
+                far(t, not straight).start()
+            if straight:
+                tile_ref[j % S, mine, :] = value
+            else:
+                tile_ref[i % S, :, mine] = value.T
+            near(t, straight).start()
+    for t, (i, j, xo, zo, slot) in enumerate(blocks):
+        straight = (xo, zo) == (j // S, i)
+        if i != j:
+            xf, zf = chip(t, not straight)
+
+            @pl.when((x == xf) & (z == zf))
+            def _():
+                far(t, not straight).wait_recv()
+                near(t, not straight).start()
+    for t, (i, j, xo, zo, slot) in enumerate(blocks):
+        straight = (xo, zo) == (j // S, i)
+        swap(t).wait_send()
+
+        @pl.when(x != xo)
+        def _():
+            cross(t).wait_send()
+
+        @pl.when((x == xo) & (z != zo))
+        def _():
+            along(t, z).wait_send()
+        for direct in ((straight, not straight) if i != j else (straight,)):
+            xn, zn = chip(t, direct)
+
+            @pl.when((x == xn) & (z == zn))
+            def _():
+                near(t, direct).wait()
+        if i != j:
+            @pl.when((x == xo) & (z == zo))
+            def _():
+                far(t, not straight).wait_send()
+    for b in range(S):
+        out[:, b * kd:(b + 1) * kd] = tile_ref[b]
+
+
+def image_kernel(R, S, Q, blocks, v, a, out, vall, img, ybuf, sbuf, ubuf, tbuf, abuf, ahi, alo, vhi, vlo,
+                 ihi, ilo, rhi, rlo, lsem, asem, os, orr, xs, xr, fs, fr, hs, hr, ts, tr,
+                 part, r_sub, r_col, r_row, flip, tile_ref, ps, pr, qs, qr, us, ur, gs, gr, es, er):
     z, x, s = lax.axis_index("row"), lax.axis_index("col"), lax.axis_index("sub")
     c = x * S + s
     m, kd = v.shape
@@ -290,17 +416,18 @@
 
     barrier = pltpu.get_barrier_semaphore()
     pl.semaphore_signal(barrier, inc=1, device_id={"sub": other}, device_id_type=MESH)
-    pl.semaphore_signal(barrier, inc=1, device_id={"col": 1 - x}, device_id_type=MESH)
+    for q in range(R):
+        if q > 0:
+            pl.semaphore_signal(barrier, inc=1, device_id={"row": lax.rem(z + q, R)}, device_id_type=MESH)
+        pl.semaphore_signal(barrier, inc=1, device_id={"col": 1 - x, "row": q}, device_id_type=MESH)
 
     @pl.when(z > 0)
     def _():
-        for t in range(S):
-            pl.semaphore_signal(barrier, inc=1, device_id={"row": z - 1, "sub": t}, device_id_type=MESH)
+        pl.semaphore_signal(barrier, inc=1, device_id={"row": z - 1, "sub": other}, device_id_type=MESH)
 
     @pl.when(z < R - 1)
     def _():
-        for t in range(S):
-            pl.semaphore_signal(barrier, inc=1, device_id={"row": z + 1, "sub": t}, device_id_type=MESH)
+        pl.semaphore_signal(barrier, inc=1, device_id={"row": z + 1, "sub": other}, device_id_type=MESH)
 
     def load(i):
         return pltpu.make_async_copy(a.at[:, rows(i, w)], abuf.at[lax.rem(i, 2)], asem.at[lax.rem(i, 2)])
@@ -339,7 +466,7 @@
     load(0).start()
     img[...] = jnp.zeros_like(img)
     ybuf[...] = jnp.zeros_like(ybuf)
-    pl.semaphore_wait(barrier, 2 + S * ((z > 0).astype(jnp.int32) + (z < R - 1).astype(jnp.int32)))
+    pl.semaphore_wait(barrier, 2 * R + (z > 0).astype(jnp.int32) + (z < R - 1).astype(jnp.int32))
     mate().start()
 
     def begin(i, carry):
@@ -518,15 +645,8 @@
     def _():
         fold(0)
 
-    for b in range(2 * S):
-        mine = slice(b * kd, (b + 1) * kd)
-        for e in range(b, 2 * S):
-            theirs = slice(e * kd, (e + 1) * kd)
-            total = ybuf[mine, theirs] + ybuf[theirs, mine].T
-            out[mine, theirs] = total
-            if e > b:
-                out[theirs, mine] = total.T
-
+    reduce_blocks(R, S, blocks, out, ybuf, part, r_sub, r_col, r_row, flip, tile_ref,
+                  ps, pr, qs, qr, us, ur, gs, gr, es, er)
     mate().wait_send()
 
     def drain(i, carry):
@@ -561,9 +681,11 @@
     half = S * kd
     dma = pltpu.SemaphoreType.DMA
     f32, bf16 = jnp.float32, jnp.bfloat16
+    blocks, most = owners(R, S)
+    nb, hr = len(blocks), kd // S
     return pl.pallas_call(
-        functools.partial(image_kernel, R, S, Q),
-        out_shape=jax.ShapeDtypeStruct((2 * half, 2 * half), f32),
+        functools.partial(image_kernel, R, S, Q, blocks),
+        out_shape=jax.ShapeDtypeStruct((kd, half), f32),
         in_specs=[pl.BlockSpec(memory_space=pltpu.VMEM), pl.BlockSpec(memory_space=pl.ANY)],
         out_specs=pl.BlockSpec(memory_space=pltpu.VMEM),
         scratch_shapes=[
@@ -576,9 +698,13 @@
             pltpu.VMEM((w, half), bf16), pltpu.VMEM((w, half), bf16),
             dma, dma((2,)), dma, dma, dma((steps,)), dma((steps,)), dma((steps,)), dma((steps,)),
             dma((steps,)), dma((steps,)), dma((steps * Q,)), dma((steps * Q,)),
+            pltpu.VMEM((nb, kd, kd), f32), pltpu.VMEM((nb, hr, kd), f32), pltpu.VMEM((nb, hr, kd), f32),
+            pltpu.VMEM((R, most, hr, kd), f32), pltpu.VMEM((nb, kd, hr), f32), pltpu.VMEM((S, kd, kd), f32),
+            dma((nb,)), dma((nb,)), dma((nb,)), dma((nb,)), dma((nb,)), dma((R, most)),
+            dma((nb,)), dma((nb,)), dma((S,)), dma((S,)),
         ],
         compiler_params=pltpu.CompilerParams(
-            collective_id=3, has_side_effects=True, vmem_limit_bytes=60_000_000),
+            collective_id=3, has_side_effects=True, vmem_limit_bytes=64_000_000),
         cost_estimate=pl.CostEstimate(flops=0, bytes_accessed=100_000_000, transcendentals=0),
         name="image",
     )(v, a)
@@ -631,10 +757,9 @@
     m, n = matrix.shape
     halves = m == n and R == X * S and X == 2 and S == 2
     if halves:
-        partial_proj = image(basis_vectors, matrix, R, S)
+        child_block = image(basis_vectors, matrix, R, S)
     else:
-        partial_proj = partial_general(matrix, basis_vectors)
-    child_block = project(partial_proj, R, X, S, halves)
+        child_block = project(partial_general(matrix, basis_vectors), R, X, S)
     row_ids = (
         jnp.arange(child_block.shape[0], dtype=jnp.int32)
         + lax.axis_index("row") * child_block.shape[0]

time: 172 us -> 163 us (0.948)
  the two profiles are of different devices: /device:TPU:3 before, /device:TPU:17 now
where the time goes in v5:
time: 163 us
  Pallas kernels  161 us (99%)
  other arithmetic  2.01 us (1%)
    pallas_call x1, Pallas kernels, image(): pl.pallas_call(functools.partial(image_kernel, R, S, Q, blocks), out_shap...  161 us

profile of v5, /device:TPU:17, one launch (start us, length us, event | category | flops | bytes accessed | tf_op | source)
XLA Modules:
  0.0 163.2 jit_solution(1763229363649835313)
XLA Ops:
  0.7 160.5 %image.1 = f32[256,512]{1,0:T(8,128)} custom-call(f32[2048,256]{1,0:T(8,128)} %v.1, f32[2048,2048]{1,0:T(8,128)} %a.1), custom_call_target="tpu_custom_call" | custom-call | bytes 100000000 | tf_op jit(solution)/shard_map/image/pallas_call | solution.py:686
  161.2 2.0 %select_bitcast_fusion = f32[1,256,512]{2,1,0:T(8,128)} fusion(f32[256,512]{1,0:T(8,128)} %image.1, pred[512]{0:T(512)(128)(4,1)S(1)} %get-tuple-element.7, pred[512]{0:T(512)(128)(4,1)S(1)} %get-tuple-element.8, pred[]{:T(512)S(6)} %eq.3, pred[256]{0:T(512)(128)(4,1)S(1)} %get-tuple-element.5, pred[256]{0:T(512)(128)(4,1)S(1)} %get-tuple-element.6), kind=kLoop, calls=%fused_computation | loop fusion | flops 524288 | bytes 1050113 | tf_op jit(solution)/shard_map/broadcast_in_dim | solution.py:777
  (2 shorter events, 0.0 us)

commit v6 on v5

--- a/solution.py
+++ b/solution.py
@@ -277,6 +277,11 @@
     mine = pl.ds(pl.multiple_of(s * hr, hr), hr)
     theirs = pl.ds(pl.multiple_of(other * hr, hr), hr)
 
+    def filled(t, side):
+        i, j = blocks[t][:2]
+        inner = z // S == side
+        return inner if side == 1 or min(i // S, j // S) > 0 else z >= 0
+
     def held(g):
         return pl.ds(pl.multiple_of((jnp.where(x == g // S, 0, 1) * S + g % S) * kd, kd), kd)
 
@@ -324,18 +329,18 @@
         swap(t).wait_recv()
         part[t, mine, :] += r_sub[t]
 
-        @pl.when(x != xo)
+        @pl.when((x != xo) & filled(t, 1 - xo))
         def _():
             cross(t).start()
     for t, (i, j, xo, zo, slot) in enumerate(blocks):
-        @pl.when(x == xo)
+        @pl.when((x == xo) & filled(t, 1 - xo))
         def _():
             cross(t).wait_recv()
             part[t, mine, :] += r_col[t]
 
-            @pl.when(z != zo)
-            def _():
-                along(t, z).start()
+        @pl.when((x == xo) & (z != zo))
+        def _():
+            along(t, z).start()
     for t, (i, j, xo, zo, slot) in enumerate(blocks):
         straight = (xo, zo) == (j // S, i)
 
@@ -367,7 +372,7 @@
         straight = (xo, zo) == (j // S, i)
         swap(t).wait_send()
 
-        @pl.when(x != xo)
+        @pl.when((x != xo) & filled(t, 1 - xo))
         def _():
             cross(t).wait_send()
 
@@ -402,8 +407,10 @@
     last = jnp.where(x == 0, R - 1, c)
     chained = (z >= first) & (z <= last)
     diag = z == c
-    pair = (z == x * S + 1) & (s == 0)
-    relay = (z == x * S) & (s == 1 - x)
+    pair = (x == 1) & (z == x * S + 1) & (s == 0)
+    catcher = (x == 0) & diag & (z == 1)
+    relay = (x == 1) & (z == x * S) & (s == 1 - x)
+    helper = (x == 0) & (z == 0) & (s == 1)
     adds = (x == 1) & chained
     weight = jnp.where(diag, 0.5, 1.0).astype(jnp.float32)
     other = 1 - s
@@ -449,7 +456,12 @@
     def hand(i):
         return pltpu.make_async_remote_copy(
             vall.at[rows(i, w), pl.ds(half, half)], ubuf.at[rows(i, w), :], hs.at[i], hr.at[i],
-            device_id={"row": z + 1, "sub": 0}, device_id_type=MESH)
+            device_id={"row": z + 1}, device_id_type=MESH)
+
+    def lift(i):
+        return pltpu.make_async_remote_copy(
+            sbuf.at[rows(i, w), :], ubuf.at[rows(i, w), :], hs.at[i], hr.at[i],
+            device_id={"row": z + 1}, device_id_type=MESH)
 
     def origin(k):
         return pltpu.make_async_remote_copy(
@@ -497,9 +509,11 @@
 
     lax.fori_loop(0, steps, prepare_own, 0)
 
-    def multiply(columns):
+    def multiply(columns, hook=None):
         def tile(t, carry):
             here = rows(t, w)
+            if hook is not None:
+                hook(t)
             img[here, columns] += dot3(ahi[here, :], alo[here, :], rhi[...], rlo[...], (1,))
             return carry
         lax.fori_loop(0, steps, tile, 0)
@@ -544,9 +558,20 @@
             ilo[rows(t, w), :] = low
             return carry
         lax.fori_loop(0, steps, halve, 0)
-        for b in range(2 * S):
-            part = slice(b * kd, (b + 1) * kd)
-            ybuf[part, columns] = dot3(vhi[:, part], vlo[:, part], ihi[...], ilo[...], (0,))
+        def act(b, carry):
+            here = rows(b, kd)
+            ybuf[here, columns] = dot3(vhi[:, here], vlo[:, here], ihi[...], ilo[...], (0,))
+            return carry
+        lax.fori_loop(0, 2 * S, act, 0)
+
+    def absorb(value, hh, i):
+        feed(value)
+
+        def act(b, carry):
+            here, columns = rows(b, kd), pl.ds(hh * half, half)
+            ybuf[here, columns] += dot3(vhi[rows(i, w), here], vlo[rows(i, w), here], rhi[...], rlo[...], (0,))
+            return carry
+        lax.fori_loop(0, 2 * S, act, 0)
 
     def local_step(i, carry):
         receive(i)
@@ -573,7 +598,7 @@
         def _():
             tbuf[...] = weight * dot3(ahi[...], alo[...], vhi[:, :half], vlo[:, :half], (0,))
 
-        def piece(p, carry):
+        def piece(p, carry, i=i):
             k = i * Q + p
 
             @pl.when(chained & (z > first))
@@ -592,9 +617,11 @@
             def _():
                 onward(k).start()
             return carry
-        lax.fori_loop(0, Q, piece, 0)
-
-        lag = jnp.where(relay, 0, steps // 2)
+        @pl.when((x == 1) | (i == 0))
+        def _():
+            lax.fori_loop(0, Q, piece, 0)
+
+        lag = steps // 2
 
         @pl.when(jnp.logical_not(diag) & (i >= lag) & (2 * (i - lag) < steps))
         def _():
@@ -604,14 +631,16 @@
         @pl.when((x == 0) & chained)
         def _():
             feed(sbuf[rows(i, w), :])
-            multiply(pl.ds(0, half))
+
+            def hook(t):
+                @pl.when((lax.rem(t, steps // Q) == 0) & (i < steps - 1))
+                def _():
+                    piece(t // (steps // Q), 0, i + 1)
+            multiply(pl.ds(0, half), hook)
 
         @pl.when((x == 1) & diag)
         def _():
-            feed(sbuf[rows(i, w), :])
-            for b in range(2 * S):
-                part = slice(b * kd, (b + 1) * kd)
-                ybuf[part, :half] += dot3(vhi[rows(i, w), part], vlo[rows(i, w), part], rhi[...], rlo[...], (0,))
+            absorb(sbuf[rows(i, w), :], 0, i)
 
         @pl.when(pair)
         def _():
@@ -633,7 +662,34 @@
         def _():
             load(0).start()
 
-    @pl.when(jnp.logical_not(source))
+    @pl.when(catcher)
+    def _():
+        def catch(i, carry):
+            lift(i).wait_recv()
+            absorb(ubuf[rows(i, w), :], 1, i)
+            return carry
+        lax.fori_loop(0, steps, catch, 0)
+
+    @pl.when(helper)
+    def _():
+        def obtain(i, carry):
+            receive(i)
+            return carry
+
+        def keep(i, carry):
+            collect(i)
+            return carry
+
+        def raise_step(i, carry):
+            open_block(i)
+            sbuf[rows(i, w), :] = dot3(ahi[...], alo[...], vhi[:, half:], vlo[:, half:], (0,))
+            lift(i).start()
+            return carry
+        lax.fori_loop(0, steps, obtain, 0)
+        lax.fori_loop(0, steps, keep, 0)
+        lax.fori_loop(0, steps, raise_step, 0)
+
+    @pl.when(jnp.logical_not(source | helper))
     def _():
         lax.fori_loop(0, steps, stream_step, 0)
 
@@ -656,6 +712,10 @@
         @pl.when(relay)
         def _():
             hand(i).wait_send()
+
+        @pl.when(helper)
+        def _():
+            lift(i).wait_send()
         return carry
 
     lax.fori_loop(0, steps, drain, 0)

time: 163 us -> 159 us (0.975)
  the two profiles are of different devices: /device:TPU:17 before, /device:TPU:3 now
where the time goes in v6:
time: 159 us; the launch traced here: 158 us
  Pallas kernels  156 us (98%)
  other arithmetic  2.01 us (1%)
    pallas_call x1, Pallas kernels, image(): pl.pallas_call(functools.partial(image_kernel, R, S, Q, blocks), out_shap...  156 us

profile of v6, /device:TPU:3, one launch (start us, length us, event | category | flops | bytes accessed | tf_op | source)
XLA Modules:
  0.0 158.3 jit_solution(1870212200627770476)
XLA Ops:
  0.7 155.6 %image.1 = f32[256,512]{1,0:T(8,128)} custom-call(f32[2048,256]{1,0:T(8,128)} %v.1, f32[2048,2048]{1,0:T(8,128)} %a.1), custom_call_target="tpu_custom_call" | custom-call | bytes 100000000 | tf_op jit(solution)/shard_map/image/pallas_call | solution.py:746
  156.3 2.0 %select_bitcast_fusion = f32[1,256,512]{2,1,0:T(8,128)} fusion(f32[256,512]{1,0:T(8,128)} %image.1, pred[512]{0:T(512)(128)(4,1)S(1)} %get-tuple-element.7, pred[512]{0:T(512)(128)(4,1)S(1)} %get-tuple-element.8, pred[]{:T(512)S(6)} %eq.3, pred[256]{0:T(512)(128)(4,1)S(1)} %get-tuple-element.5, pred[256]{0:T(512)(128)(4,1)S(1)} %get-tuple-element.6), kind=kLoop, calls=%fused_computation | loop fusion | flops 524288 | bytes 1050113 | tf_op jit(solution)/shard_map/broadcast_in_dim | solution.py:837
  (2 shorter events, 0.0 us)

commit v7 on v6

--- a/solution.py
+++ b/solution.py
@@ -394,7 +394,7 @@
 
 
 def image_kernel(R, S, Q, blocks, v, a, out, vall, img, ybuf, sbuf, ubuf, tbuf, abuf, ahi, alo, vhi, vlo,
-                 ihi, ilo, rhi, rlo, lsem, asem, os, orr, xs, xr, fs, fr, hs, hr, ts, tr,
+                 ihi, ilo, rhi, rlo, whi, wlo, lsem, asem, os, orr, xs, xr, fs, fr, hs, hr, ts, tr,
                  part, r_sub, r_col, r_row, flip, tile_ref, ps, pr, qs, qr, us, ur, gs, gr, es, er):
     z, x, s = lax.axis_index("row"), lax.axis_index("col"), lax.axis_index("sub")
     c = x * S + s
@@ -509,11 +509,9 @@
 
     lax.fori_loop(0, steps, prepare_own, 0)
 
-    def multiply(columns, hook=None):
+    def multiply(columns):
         def tile(t, carry):
             here = rows(t, w)
-            if hook is not None:
-                hook(t)
             img[here, columns] += dot3(ahi[here, :], alo[here, :], rhi[...], rlo[...], (1,))
             return carry
         lax.fori_loop(0, steps, tile, 0)
@@ -574,7 +572,13 @@
         lax.fori_loop(0, 2 * S, act, 0)
 
     def local_step(i, carry):
-        receive(i)
+        @pl.when(i == 0)
+        def _():
+            receive(i)
+
+        @pl.when(i < steps - 1)
+        def _():
+            receive(i + 1)
         open_block(i)
 
         @pl.when(x == 0)
@@ -586,25 +590,12 @@
         multiply(pl.ds(half, half))
         return carry
 
-    def stream_step(i, carry):
-        @pl.when(jnp.logical_not(diag) & (2 * i < steps))
-        def _():
-            receive(2 * i)
-            receive(2 * i + 1)
-
-        open_block(i)
-
-        @pl.when(adds)
-        def _():
-            tbuf[...] = weight * dot3(ahi[...], alo[...], vhi[:, :half], vlo[:, :half], (0,))
-
-        def piece(p, carry, i=i):
-            k = i * Q + p
-
-            @pl.when(chained & (z > first))
-            def _():
-                onward(k).wait_recv()
-
+    def piece(k, p, adding):
+        @pl.when(chained & (z > first))
+        def _():
+            onward(k).wait_recv()
+
+        if adding:
             @pl.when(adds & (z == first))
             def _():
                 sbuf[rows(k, pw), :] = tbuf[rows(p, pw), :]
@@ -613,13 +604,26 @@
             def _():
                 sbuf[rows(k, pw), :] += tbuf[rows(p, pw), :]
 
-            @pl.when(chained & (z < last))
-            def _():
-                onward(k).start()
-            return carry
-        @pl.when((x == 1) | (i == 0))
-        def _():
-            lax.fori_loop(0, Q, piece, 0)
+        @pl.when(chained & (z < last))
+        def _():
+            onward(k).start()
+
+    def stream_step(i, carry):
+        @pl.when(jnp.logical_not(diag) & (2 * i < steps))
+        def _():
+            receive(2 * i)
+            receive(2 * i + 1)
+
+        open_block(i)
+
+        @pl.when(adds)
+        def _():
+            tbuf[...] = weight * dot3(ahi[...], alo[...], vhi[:, :half], vlo[:, :half], (0,))
+
+        def next_piece(p, c2):
+            piece(i * Q + p, p, True)
+            return c2
+        lax.fori_loop(0, Q, next_piece, 0)
 
         lag = steps // 2
 
@@ -628,25 +632,51 @@
             collect(2 * (i - lag))
             collect(2 * (i - lag) + 1)
 
-        @pl.when((x == 0) & chained)
-        def _():
-            feed(sbuf[rows(i, w), :])
-
-            def hook(t):
-                @pl.when((lax.rem(t, steps // Q) == 0) & (i < steps - 1))
-                def _():
-                    piece(t // (steps // Q), 0, i + 1)
-            multiply(pl.ds(0, half), hook)
-
-        @pl.when((x == 1) & diag)
+        @pl.when(diag)
         def _():
             absorb(sbuf[rows(i, w), :], 0, i)
-
-        @pl.when(pair)
-        def _():
-            hand(i).wait_recv()
-            feed(ubuf[rows(i, w), :])
-            multiply(pl.ds(half, half))
+        return carry
+
+    def early_step(i, carry):
+        receive(2 * i)
+        receive(2 * i + 1)
+
+        def next_piece(p, c2):
+            piece(i * Q + p, p, False)
+            return c2
+        lax.fori_loop(0, Q, next_piece, 0)
+        return carry
+
+    def wide_step(n, carry):
+        open_block(n)
+
+        def widen(b, c2):
+            here = rows(b, kd)
+            high, low = split(dot3(vhi[:, here], vlo[:, here], ahi[...], alo[...], (0,)))
+            whi[here, :] = high
+            wlo[here, :] = low
+
+            @pl.when(lax.rem(b, 2) == 0)
+            def _():
+                piece(steps // 2 * Q + n * (Q // 2) + b // 2, 0, False)
+            return c2
+        lax.fori_loop(0, 2 * S, widen, 0)
+
+        @pl.when(x == 0)
+        def _():
+            feed(sbuf[rows(n, w), :])
+
+        @pl.when(x == 1)
+        def _():
+            hand(n).wait_recv()
+            feed(ubuf[rows(n, w), :])
+        columns = rows(x, half)
+
+        def add(b, c2):
+            here = rows(b, kd)
+            ybuf[here, columns] += dot3(whi[here, :], wlo[here, :], rhi[...], rlo[...], (1,))
+            return c2
+        lax.fori_loop(0, 2 * S, add, 0)
         return carry
 
     @pl.when(diag)
@@ -689,17 +719,20 @@
         lax.fori_loop(0, steps, keep, 0)
         lax.fori_loop(0, steps, raise_step, 0)
 
-    @pl.when(jnp.logical_not(source | helper))
+    wide = pair | ((x == 0) & chained & jnp.logical_not(diag))
+
+    @pl.when(wide)
+    def _():
+        def keep_all(i, carry):
+            collect(i)
+            return carry
+        lax.fori_loop(0, steps // 2, early_step, 0)
+        lax.fori_loop(0, steps, keep_all, 0)
+        lax.fori_loop(0, steps, wide_step, 0)
+
+    @pl.when((x == 1) & jnp.logical_not(pair))
     def _():
         lax.fori_loop(0, steps, stream_step, 0)
-
-    @pl.when(pair)
-    def _():
-        fold(1)
-
-    @pl.when((x == 0) & chained & jnp.logical_not(diag))
-    def _():
-        fold(0)
 
     reduce_blocks(R, S, blocks, out, ybuf, part, r_sub, r_col, r_row, flip, tile_ref,
                   ps, pr, qs, qr, us, ur, gs, gr, es, er)
@@ -756,6 +789,7 @@
             pltpu.VMEM((m, 2 * half), bf16), pltpu.VMEM((m, 2 * half), bf16),
             pltpu.VMEM((m, half), bf16), pltpu.VMEM((m, half), bf16),
             pltpu.VMEM((w, half), bf16), pltpu.VMEM((w, half), bf16),
+            pltpu.VMEM((2 * half, w), bf16), pltpu.VMEM((2 * half, w), bf16),
             dma, dma((2,)), dma, dma, dma((steps,)), dma((steps,)), dma((steps,)), dma((steps,)),
             dma((steps,)), dma((steps,)), dma((steps * Q,)), dma((steps * Q,)),
             pltpu.VMEM((nb, kd, kd), f32), pltpu.VMEM((nb, hr, kd), f32), pltpu.VMEM((nb, hr, kd), f32),

time: 159 us -> 159 us (level)
  no operation moved by 1% of the time
where the time goes in v7:
time: 159 us
  Pallas kernels  156 us (98%)
  other arithmetic  2.01 us (1%)
    pallas_call x1, Pallas kernels, image(): pl.pallas_call(functools.partial(image_kernel, R, S, Q, blocks), out_shap...  156 us

profile of v7, /device:TPU:3, one launch (start us, length us, event | category | flops | bytes accessed | tf_op | source)
XLA Modules:
  0.0 158.7 jit_solution(14604767926349132485)
XLA Ops:
  0.7 156.1 %image.1 = f32[256,512]{1,0:T(8,128)} custom-call(f32[2048,256]{1,0:T(8,128)} %v.1, f32[2048,2048]{1,0:T(8,128)} %a.1), custom_call_target="tpu_custom_call" | custom-call | bytes 100000000 | tf_op jit(solution)/shard_map/image/pallas_call | solution.py:779
  156.8 2.0 %select_bitcast_fusion = f32[1,256,512]{2,1,0:T(8,128)} fusion(f32[256,512]{1,0:T(8,128)} %image.1, pred[512]{0:T(512)(128)(4,1)S(1)} %get-tuple-element.7, pred[512]{0:T(512)(128)(4,1)S(1)} %get-tuple-element.8, pred[]{:T(512)S(6)} %eq.3, pred[256]{0:T(512)(128)(4,1)S(1)} %get-tuple-element.5, pred[256]{0:T(512)(128)(4,1)S(1)} %get-tuple-element.6), kind=kLoop, calls=%fused_computation | loop fusion | flops 524288 | bytes 1050113 | tf_op jit(solution)/shard_map/broadcast_in_dim | solution.py:871
  (2 shorter events, 0.0 us)

commit v8 on v7

--- a/solution.py
+++ b/solution.py
@@ -590,23 +590,30 @@
         multiply(pl.ds(half, half))
         return carry
 
-    def piece(k, p, adding):
+    def piece(k, p=0, buffer=None):
         @pl.when(chained & (z > first))
         def _():
             onward(k).wait_recv()
 
-        if adding:
+        if buffer is not None:
             @pl.when(adds & (z == first))
             def _():
-                sbuf[rows(k, pw), :] = tbuf[rows(p, pw), :]
+                sbuf[rows(k, pw), :] = tbuf[buffer, rows(p, pw), :]
 
             @pl.when(adds & (z > first))
             def _():
-                sbuf[rows(k, pw), :] += tbuf[rows(p, pw), :]
+                sbuf[rows(k, pw), :] += tbuf[buffer, rows(p, pw), :]
 
         @pl.when(chained & (z < last))
         def _():
             onward(k).start()
+
+    def own_tile(i):
+        open_block(i)
+
+        @pl.when(adds)
+        def _():
+            tbuf[lax.rem(i, 2)] = weight * dot3(ahi[...], alo[...], vhi[:, :half], vlo[:, :half], (0,))
 
     def stream_step(i, carry):
         @pl.when(jnp.logical_not(diag) & (2 * i < steps))
@@ -614,14 +621,12 @@
             receive(2 * i)
             receive(2 * i + 1)
 
-        open_block(i)
-
-        @pl.when(adds)
-        def _():
-            tbuf[...] = weight * dot3(ahi[...], alo[...], vhi[:, :half], vlo[:, :half], (0,))
+        @pl.when(i < steps - 1)
+        def _():
+            own_tile(i + 1)
 
         def next_piece(p, c2):
-            piece(i * Q + p, p, True)
+            piece(i * Q + p, p, lax.rem(i, 2))
             return c2
         lax.fori_loop(0, Q, next_piece, 0)
 
@@ -637,12 +642,18 @@
             absorb(sbuf[rows(i, w), :], 0, i)
         return carry
 
+    early = jnp.where((x == 0) & (z == 1), steps, 3 * steps // 8)
+    left = (steps - early) * Q
+    turns = steps * 2 * S
+
     def early_step(i, carry):
-        receive(2 * i)
-        receive(2 * i + 1)
+        @pl.when(2 * i < steps)
+        def _():
+            receive(2 * i)
+            receive(2 * i + 1)
 
         def next_piece(p, c2):
-            piece(i * Q + p, p, False)
+            piece(i * Q + p)
             return c2
         lax.fori_loop(0, Q, next_piece, 0)
         return carry
@@ -656,9 +667,11 @@
             whi[here, :] = high
             wlo[here, :] = low
 
-            @pl.when(lax.rem(b, 2) == 0)
+            turn = n * 2 * S + b
+
+            @pl.when((turn + 1) * left // turns > turn * left // turns)
             def _():
-                piece(steps // 2 * Q + n * (Q // 2) + b // 2, 0, False)
+                piece(early * Q + turn * left // turns)
             return c2
         lax.fori_loop(0, 2 * S, widen, 0)
 
@@ -726,12 +739,18 @@
         def keep_all(i, carry):
             collect(i)
             return carry
-        lax.fori_loop(0, steps // 2, early_step, 0)
+        lax.fori_loop(0, early, early_step, 0)
+
+        def rest(i, carry):
+            receive(i)
+            return carry
+        lax.fori_loop(jnp.minimum(2 * early, steps), steps, rest, 0)
         lax.fori_loop(0, steps, keep_all, 0)
         lax.fori_loop(0, steps, wide_step, 0)
 
     @pl.when((x == 1) & jnp.logical_not(pair))
     def _():
+        own_tile(0)
         lax.fori_loop(0, steps, stream_step, 0)
 
     reduce_blocks(R, S, blocks, out, ybuf, part, r_sub, r_col, r_row, flip, tile_ref,
@@ -784,7 +803,7 @@
         scratch_shapes=[
             pltpu.VMEM((m, 2 * half), f32), pltpu.VMEM((m, 2 * half), f32),
             pltpu.VMEM((2 * half, 2 * half), f32),
-            pltpu.VMEM((m, half), f32), pltpu.VMEM((m, half), f32), pltpu.VMEM((w, half), f32),
+            pltpu.VMEM((m, half), f32), pltpu.VMEM((m, half), f32), pltpu.VMEM((2, w, half), f32),
             pltpu.VMEM((2, m, w), f32), pltpu.VMEM((m, w), bf16), pltpu.VMEM((m, w), bf16),
             pltpu.VMEM((m, 2 * half), bf16), pltpu.VMEM((m, 2 * half), bf16),
             pltpu.VMEM((m, half), bf16), pltpu.VMEM((m, half), bf16),
@@ -798,7 +817,7 @@
             dma((nb,)), dma((nb,)), dma((S,)), dma((S,)),
         ],
         compiler_params=pltpu.CompilerParams(
-            collective_id=3, has_side_effects=True, vmem_limit_bytes=64_000_000),
+            collective_id=3, has_side_effects=True, vmem_limit_bytes=66_000_000),
         cost_estimate=pl.CostEstimate(flops=0, bytes_accessed=100_000_000, transcendentals=0),
         name="image",
     )(v, a)

time: 159 us -> 158 us (level)
  no operation moved by 1% of the time
where the time goes in v8:
time: 158 us
  Pallas kernels  155 us (98%)
  other arithmetic  2.01 us (1%)
    pallas_call x1, Pallas kernels, image(): pl.pallas_call(functools.partial(image_kernel, R, S, Q, blocks), out_shap...  155 us

profile of v8, /device:TPU:3, one launch (start us, length us, event | category | flops | bytes accessed | tf_op | source)
XLA Modules:
  0.0 157.8 jit_solution(10956776761450637535)
XLA Ops:
  0.7 155.1 %image.1 = f32[256,512]{1,0:T(8,128)} custom-call(f32[2048,256]{1,0:T(8,128)} %v.1, f32[2048,2048]{1,0:T(8,128)} %a.1), custom_call_target="tpu_custom_call" | custom-call | bytes 100000000 | tf_op jit(solution)/shard_map/image/pallas_call | solution.py:798
  155.8 2.0 %select_bitcast_fusion = f32[1,256,512]{2,1,0:T(8,128)} fusion(f32[256,512]{1,0:T(8,128)} %image.1, pred[512]{0:T(512)(128)(4,1)S(1)} %get-tuple-element.7, pred[512]{0:T(512)(128)(4,1)S(1)} %get-tuple-element.8, pred[]{:T(512)S(6)} %eq.3, pred[256]{0:T(512)(128)(4,1)S(1)} %get-tuple-element.5, pred[256]{0:T(512)(128)(4,1)S(1)} %get-tuple-element.6), kind=kLoop, calls=%fused_computation | loop fusion | flops 524288 | bytes 1050113 | tf_op jit(solution)/shard_map/broadcast_in_dim | solution.py:890
  (2 shorter events, 0.0 us)

commit v9 on v8

--- a/solution.py
+++ b/solution.py
@@ -476,8 +476,6 @@
     own = pltpu.make_async_copy(v, vall.at[:, block(0, s)], lsem)
     own.start()
     load(0).start()
-    img[...] = jnp.zeros_like(img)
-    ybuf[...] = jnp.zeros_like(ybuf)
     pl.semaphore_wait(barrier, 2 * R + (z > 0).astype(jnp.int32) + (z < R - 1).astype(jnp.int32))
     mate().start()
 
@@ -486,6 +484,8 @@
         return carry
 
     lax.fori_loop(0, steps, begin, 0)
+    img[...] = jnp.zeros_like(img)
+    ybuf[...] = jnp.zeros_like(ybuf)
     own.wait()
     mate().wait_recv()
     source = (x == 0) & diag

time: 158 us -> 158 us (level)
  no operation moved by 1% of the time
where the time goes in v9:
time: 158 us
  Pallas kernels  155 us (98%)
  other arithmetic  2.01 us (1%)
    pallas_call x1, Pallas kernels, image(): pl.pallas_call(functools.partial(image_kernel, R, S, Q, blocks), out_shap...  155 us

profile of v9, /device:TPU:3, one launch (start us, length us, event | category | flops | bytes accessed | tf_op | source)
XLA Modules:
  0.0 157.8 jit_solution(2256205147983059794)
XLA Ops:
  0.7 155.1 %image.1 = f32[256,512]{1,0:T(8,128)} custom-call(f32[2048,256]{1,0:T(8,128)} %v.1, f32[2048,2048]{1,0:T(8,128)} %a.1), custom_call_target="tpu_custom_call" | custom-call | bytes 100000000 | tf_op jit(solution)/shard_map/image/pallas_call | solution.py:798
  155.8 2.0 %select_bitcast_fusion = f32[1,256,512]{2,1,0:T(8,128)} fusion(f32[256,512]{1,0:T(8,128)} %image.1, pred[512]{0:T(512)(128)(4,1)S(1)} %get-tuple-element.7, pred[512]{0:T(512)(128)(4,1)S(1)} %get-tuple-element.8, pred[]{:T(512)S(6)} %eq.3, pred[256]{0:T(512)(128)(4,1)S(1)} %get-tuple-element.5, pred[256]{0:T(512)(128)(4,1)S(1)} %get-tuple-element.6), kind=kLoop, calls=%fused_computation | loop fusion | flops 524288 | bytes 1050113 | tf_op jit(solution)/shard_map/broadcast_in_dim | solution.py:890
  (2 shorter events, 0.0 us)
